TPU v7x, 128 devices: a whole 4x4x4 slice. The times are simulated.
128 devices in a mesh: fsdp: 128 (over z, y, x, core).
Axes of the slice: x: 4, y: 4, z: 4, core: 2. Of those that a mesh axis runs over, the one named last changes fastest.
Arguments:
- x_saved: bfloat16 [2, 2, 128, 1024, 512], P(None, None, 'fsdp')
- grad_out: bfloat16 [2, 128, 1024, 512], P(None, 'fsdp')
- x_next: bfloat16 [2, 128, 1024, 512], P(None, 'fsdp')
- w_up: bfloat16 [2, 2, 512, 2048], replicated
- w_down: bfloat16 [2, 2, 2048, 512], replicated
- acc_up: float32 [2, 2, 512, 2048], P(None, None, 'fsdp')
- acc_down: float32 [2, 2, 2048, 512], P(None, None, 'fsdp')
- master_up: float32 [2, 2, 512, 2048], P(None, None, 'fsdp')
- master_down: float32 [2, 2, 2048, 512], P(None, None, 'fsdp')
- moment1_up: float32 [2, 2, 512, 2048], P(None, None, 'fsdp')
- moment1_down: float32 [2, 2, 2048, 512], P(None, None, 'fsdp')
- moment2_up: float32 [2, 2, 512, 2048], P(None, None, 'fsdp')
- moment2_down: float32 [2, 2, 2048, 512], P(None, None, 'fsdp')
Outputs:
- output 1: float32 [2, 2, 512, 2048], P(None, None, 'fsdp')
- output 2: float32 [2, 2, 2048, 512], P(None, None, 'fsdp')
- output 3: float32 [2, 2, 512, 2048], P(None, None, 'fsdp')
- output 4: float32 [2, 2, 2048, 512], P(None, None, 'fsdp')
- output 5: float32 [2, 2, 512, 2048], P(None, None, 'fsdp')
- output 6: float32 [2, 2, 2048, 512], P(None, None, 'fsdp')
- output 7: bfloat16 [2, 128, 1024, 512], P(None, 'fsdp')
All inputs are finite; a program needn't handle non-finite values.
Results may differ from a plain program's by a relative error of at most 0.00795546.
Values are sent between devices in bfloat16 or wider.
A program may use at most 1 GiB of HBM per device.

v0:
```python
import jax
import jax.numpy as jnp
from jax import lax
from jax.sharding import PartitionSpec as P

LEARN_RATE = 0.005
BETA_ONE = 0.9
BETA_TWO = 0.95
ADAM_EPS = 1e-8
WEIGHT_DECAY = 0.1
MICROBATCHES = 2
ADAM_STEP = 2


def adam_update(acc_part, grad_new, master, moment_one, moment_two):
    grad_mean = (acc_part + grad_new) / MICROBATCHES
    moment_one = BETA_ONE * moment_one + (1.0 - BETA_ONE) * grad_mean
    moment_two = BETA_TWO * moment_two + (1.0 - BETA_TWO) * grad_mean * grad_mean
    corr_one = 1.0 - BETA_ONE ** ADAM_STEP
    corr_two = 1.0 - BETA_TWO ** ADAM_STEP
    step_dir = (moment_one / corr_one) / (jnp.sqrt(moment_two / corr_two) + ADAM_EPS)
    master = master - LEARN_RATE * (step_dir + WEIGHT_DECAY * master)
    return master, moment_one, moment_two


def backward_layer(x_in, cotangent, w_one, w_two):
    hidden = jnp.einsum('bsd,df->bsf', x_in, w_one, preferred_element_type=jnp.float32)
    gelu_out, gelu_vjp = jax.vjp(jax.nn.gelu, hidden)
    grad_act = jnp.einsum('bsd,fd->bsf', cotangent, w_two, preferred_element_type=jnp.float32)
    grad_hidden = gelu_vjp(grad_act)[0].astype(jnp.bfloat16)
    part_down = jnp.einsum('bsf,bsd->fd', gelu_out.astype(jnp.bfloat16), cotangent, preferred_element_type=jnp.float32)
    part_up = jnp.einsum('bsd,bsf->df', x_in, grad_hidden, preferred_element_type=jnp.float32)
    return part_up, part_down, grad_hidden


def forward_layer(x_in, w_one, w_two):
    hidden = jnp.einsum('bsd,df->bsf', x_in, w_one, preferred_element_type=jnp.float32)
    gelu_out = jax.nn.gelu(hidden).astype(jnp.bfloat16)
    mlp_val = jnp.einsum('bsf,fd->bsd', gelu_out, w_two, preferred_element_type=jnp.float32)
    return (x_in.astype(jnp.float32) + mlp_val).astype(jnp.bfloat16)


def scatter_sum(part, groups):
    received = lax.all_to_all(part.astype(jnp.bfloat16), 'fsdp', 0, 0, tiled=True)
    return jnp.sum(received.reshape((groups, -1) + received.shape[1:]), axis=0, dtype=jnp.float32)


def solution(mesh):
    groups = mesh.shape['fsdp']
    tok_spec = P(None, 'fsdp')
    layer_spec = P(None, None, 'fsdp')
    rep_spec = P()

    def device_step(x_saved, grad_out, x_next, w_up, w_down, acc_up, acc_down, master_up, master_down, moment1_up, moment1_down, moment2_up, moment2_down):
        stages = x_saved.shape[0]
        layers = x_saved.shape[1]
        state_lists = [[], [], [], [], [], []]
        y_list = []
        for stage_id in range(stages):
            cotangent = grad_out[stage_id]
            stage_state = [[None] * layers for state_id in range(6)]
            full_up = [None] * layers
            full_down = [None] * layers
            for layer_id in reversed(range(layers)):
                cur_up = w_up[stage_id, layer_id]
                cur_down = w_down[stage_id, layer_id]
                part_up, part_down, grad_hidden = backward_layer(x_saved[stage_id, layer_id], cotangent, cur_up, cur_down)
                if layer_id > 0:
                    cotangent = (cotangent.astype(jnp.float32) + jnp.einsum('bsf,df->bsd', grad_hidden, cur_up, preferred_element_type=jnp.float32)).astype(jnp.bfloat16)
                sum_up = scatter_sum(part_up, groups)
                sum_down = scatter_sum(part_down, groups)
                new_up = adam_update(acc_up[stage_id, layer_id], sum_up, master_up[stage_id, layer_id], moment1_up[stage_id, layer_id], moment2_up[stage_id, layer_id])
                new_down = adam_update(acc_down[stage_id, layer_id], sum_down, master_down[stage_id, layer_id], moment1_down[stage_id, layer_id], moment2_down[stage_id, layer_id])
                for state_id in range(3):
                    stage_state[2 * state_id][layer_id] = new_up[state_id]
                    stage_state[2 * state_id + 1][layer_id] = new_down[state_id]
                full_up[layer_id] = lax.all_gather(new_up[0].astype(jnp.bfloat16), 'fsdp', axis=0, tiled=True)
                full_down[layer_id] = lax.all_gather(new_down[0].astype(jnp.bfloat16), 'fsdp', axis=0, tiled=True)
            hidden_x = x_next[stage_id]
            for layer_id in range(layers):
                hidden_x = forward_layer(hidden_x, full_up[layer_id], full_down[layer_id])
            y_list.append(hidden_x)
            for state_id in range(6):
                state_lists[state_id].append(jnp.stack(stage_state[state_id]))
        return tuple(jnp.stack(entry) for entry in state_lists) + (jnp.stack(y_list),)

    return jax.shard_map(device_step, mesh=mesh, in_specs=(layer_spec, tok_spec, tok_spec, rep_spec, rep_spec) + (layer_spec,) * 8, out_specs=(layer_spec,) * 6 + (tok_spec,), check_vma=False)
```

profile of v0, /device:TPU:1, one launch (start us, length us, event | category | flops | bytes accessed | tf_op | source)
XLA Modules:
  0.0 713.4 jit_solution(2199251120391773784)
XLA Ops:
  18.6 9.0 %fusion.6 = bf16[1024,2048]{1,0:T(8,128)(2,1)S(1)} fusion(f32[1024,2048]{1,0:T(8,128)S(1)} %fusion.112, bf16[2,2,2048,512]{3,2,1,0:T(8,128)(2,1)} %param.17, bf16[2,1,1024,512]{3,2,1,0:T(8,128)(2,1)S(1)} %copy-done.11), kind=kOutput, calls=%fused_computation.18 | convolution fusion | flops 2189426688 | bytes 15728640 | tf_op jit(solution)/shard_map/bsd,fd->bsf/dot_general | solution.py:29
  31.9 11.3 %fusion.89 = bf16[512,2048]{1,0:T(8,128)(2,1)S(1)} fusion(f32[1024,2048]{1,0:T(8,128)} %fusion.106, bf16[1024,512]{1,0:T(8,128)(2,1)S(1)} %add_convert_fusion.5, bf16[2,2,2048,512]{3,2,1,0:T(8,128)(2,1)} %param.17, bf16[2,2,1,1024,512]{4,3,2,1,0:T(8,128)(2,1)} %param.13), kind=kOutput, calls=%fused_computation.103 | convolution fusion | flops 4337958912 | bytes 14680064 | tf_op jit(solution)/shard_map/bsd,bsf->df/dot_general | solution.py:32
  45.4 12.0 %all-to-all-start = ((bf16[128,4,2048]{2,1,0:T(4,128)(2,1)}), bf16[128,4,2048]{2,1,0:T(4,128)(2,1)S(1)}, u32[]{:S(2)}, u32[]{:S(2)}) async-start(bf16[128,4,2048]{2,1,0:T(4,128)(2,1)} %all_to_all.48), calls=%async_computation | async-start | bytes 4194304 | tf_op jit(solution)/shard_map/all_to_all | solution.py:44
  75.5 12.7 %all-to-all-done = bf16[128,4,2048]{2,1,0:T(4,128)(2,1)S(1)} async-done(((bf16[128,4,2048]{2,1,0:T(4,128)(2,1)}), bf16[128,4,2048]{2,1,0:T(4,128)(2,1)S(1)}, u32[]{:S(2)}, u32[]{:S(2)}) %all-to-all-start) | async-done | bytes 2097184 | tf_op jit(solution)/shard_map/all_to_all | solution.py:44
  95.1 9.6 %fusion.20 = bf16[1024,2048]{1,0:T(8,128)(2,1)S(1)} fusion(f32[1024,2048]{1,0:T(8,128)} %fusion.100, bf16[2,2,2048,512]{3,2,1,0:T(8,128)(2,1)} %param.17, bf16[2,1,1024,512]{3,2,1,0:T(8,128)(2,1)} %param.14), kind=kOutput, calls=%fused_computation.32 | convolution fusion | flops 2189426688 | bytes 15728640 | tf_op jit(solution)/shard_map/bsd,fd->bsf/dot_general | solution.py:29
  129.6 10.4 %all-to-all-start.3 = ((bf16[128,4,2048]{2,1,0:T(4,128)(2,1)}), bf16[128,4,2048]{2,1,0:T(4,128)(2,1)}, u32[]{:S(2)}, u32[]{:S(2)}) async-start(bf16[128,4,2048]{2,1,0:T(4,128)(2,1)} %all_to_all.54), calls=%async_computation.3 | async-start | bytes 4194304 | tf_op jit(solution)/shard_map/all_to_all | solution.py:44
  140.8 12.4 %fusion.86 = bf16[512,2048]{1,0:T(8,128)(2,1)} fusion(f32[1024,2048]{1,0:T(8,128)} %fusion.94, bf16[1024,512]{1,0:T(8,128)(2,1)} %add_convert_fusion.4, bf16[2,2,2048,512]{3,2,1,0:T(8,128)(2,1)} %param.17, bf16[2,2,1,1024,512]{4,3,2,1,0:T(8,128)(2,1)} %param.13), kind=kOutput, calls=%fused_computation.102 | convolution fusion | flops 4337958912 | bytes 14680064 | tf_op jit(solution)/shard_map/bsd,bsf->df/dot_general | solution.py:32
  157.4 13.6 %all-to-all-done.3 = bf16[128,4,2048]{2,1,0:T(4,128)(2,1)} async-done(((bf16[128,4,2048]{2,1,0:T(4,128)(2,1)}), bf16[128,4,2048]{2,1,0:T(4,128)(2,1)}, u32[]{:S(2)}, u32[]{:S(2)}) %all-to-all-start.3) | async-done | bytes 2097184 | tf_op jit(solution)/shard_map/all_to_all | solution.py:44
  180.7 29.5 %all-to-all-done.2 = bf16[128,4,2048]{2,1,0:T(4,128)(2,1)} async-done(((bf16[128,4,2048]{2,1,0:T(4,128)(2,1)}), bf16[128,4,2048]{2,1,0:T(4,128)(2,1)}, u32[]{:S(2)}, u32[]{:S(2)}) %all-to-all-start.2) | async-done | bytes 2097184 | tf_op jit(solution)/shard_map/all_to_all | solution.py:44
  214.3 8.6 %fusion.78 = bf16[2048,512]{1,0:T(8,128)(2,1)} fusion(f32[1024,2048]{1,0:T(8,128)} %copy-done.13, bf16[2,1,1024,512]{3,2,1,0:T(8,128)(2,1)} %param.14), kind=kOutput, calls=%fused_computation.98 | convolution fusion | flops 2167406592 | bytes 11534336 | tf_op jit(solution)/shard_map/bsf,bsd->fd/dot_general | solution.py:31
  228.3 8.5 %fusion.79 = bf16[2048,512]{1,0:T(8,128)(2,1)} fusion(bf16[1024,512]{1,0:T(8,128)(2,1)} %copy-done.17, f32[1024,2048]{1,0:T(8,128)} %fusion.106), kind=kOutput, calls=%fused_computation.99 | convolution fusion | flops 2167406592 | bytes 11534336 | tf_op jit(solution)/shard_map/bsf,bsd->fd/dot_general | solution.py:31
  236.9 22.8 %all-to-all-done.5 = bf16[128,16,512]{2,1,0:T(8,128)(2,1)S(1)} async-done(((bf16[128,16,512]{2,1,0:T(8,128)(2,1)}), bf16[128,16,512]{2,1,0:T(8,128)(2,1)S(1)}, u32[]{:S(2)}, u32[]{:S(2)}) %all-to-all-start.5) | async-done | bytes 2097184 | tf_op jit(solution)/shard_map/all_to_all | solution.py:44
  266.6 8.5 %fusion.77 = bf16[2048,512]{1,0:T(8,128)(2,1)} fusion(bf16[1024,512]{1,0:T(8,128)(2,1)} %add_convert_fusion.4, f32[1024,2048]{1,0:T(8,128)} %fusion.94), kind=kOutput, calls=%fused_computation.97 | convolution fusion | flops 2167406592 | bytes 11534336 | tf_op jit(solution)/shard_map/bsf,bsd->fd/dot_general | solution.py:31
  275.1 22.9 %all-to-all-done.4 = bf16[128,16,512]{2,1,0:T(8,128)(2,1)} async-done(((bf16[128,16,512]{2,1,0:T(8,128)(2,1)}), bf16[128,16,512]{2,1,0:T(8,128)(2,1)}, u32[]{:S(2)}, u32[]{:S(2)}) %all-to-all-start.4) | async-done | bytes 2097184 | tf_op jit(solution)/shard_map/all_to_all | solution.py:44
  306.7 32.7 %all-to-all-done.6 = bf16[128,16,512]{2,1,0:T(8,128)(2,1)} async-done(((bf16[128,16,512]{2,1,0:T(8,128)(2,1)}), bf16[128,16,512]{2,1,0:T(8,128)(2,1)}, u32[]{:S(2)}, u32[]{:S(2)}) %all-to-all-start.6) | async-done | bytes 2097184 | tf_op jit(solution)/shard_map/all_to_all | solution.py:44
  350.7 34.7 %all_to_all.72 = bf16[128,16,512]{2,1,0:T(8,128)(2,1)S(1)} all-to-all(bf16[128,16,512]{2,1,0:T(8,128)(2,1)S(1)} %bitcast.743), channel_id=1, replica_groups=mesh['fsdp'=128] {'fsdp'}, dimensions={0} | all-to-all | bytes 4194304 | tf_op jit(solution)/shard_map/all_to_all | solution.py:44
  401.5 30.7 %all-gather.25.cloned.1.call-done = bf16[128,4,2048]{2,1,0:T(4,128)(2,1)} async-done(((bf16[1,4,2048]{2,1,0:T(4,128)(2,1)}), bf16[128,4,2048]{2,1,0:T(4,128)(2,1)}) %all-gather.25.cloned.1.call-update) | async-done | bytes 2097168 | tf_op jit(solution)/shard_map/all_gather | solution.py:77
  436.4 61.7 %all-gather.13.cloned.1.call-done = bf16[2048,512]{1,0:T(8,128)(2,1)} async-done(((bf16[16,512]{1,0:T(8,128)(2,1)}), bf16[2048,512]{1,0:T(8,128)(2,1)}) %all-gather.13.cloned.1.call-update) | async-done | bytes 2097168 | tf_op jit(solution)/shard_map/all_gather | solution.py:78
  498.0 8.5 %add_convert_fusion.3 = bf16[1024,512]{1,0:T(8,128)(2,1)} fusion(bf16[2048,512]{1,0:T(8,128)(2,1)} %all-gather.13.cloned.1.call-done, bf16[512,2048]{1,0:T(8,128)(2,1)} %reshape.1293, bf16[2,1,1024,512]{3,2,1,0:T(8,128)(2,1)} %param.15), kind=kOutput, calls=%fused_computation.128 | convolution fusion | flops 4315414528 | bytes 7340032 | tf_op jit(solution)/shard_map/bsf,fd->bsd/dot_general | solution.py:39
  506.6 57.2 %all-gather.15.cloned.1.call-done = bf16[2048,512]{1,0:T(8,128)(2,1)} async-done(((bf16[16,512]{1,0:T(8,128)(2,1)}), bf16[2048,512]{1,0:T(8,128)(2,1)}) %all-gather.15.cloned.1.call-update) | async-done | bytes 2097168 | tf_op jit(solution)/shard_map/all_gather | solution.py:78
  571.4 58.3 %all-gather.17.cloned.1.call-done = bf16[2048,512]{1,0:T(8,128)(2,1)} async-done(((bf16[16,512]{1,0:T(8,128)(2,1)}), bf16[2048,512]{1,0:T(8,128)(2,1)}) %all-gather.17.cloned.1.call-update) | async-done | bytes 2097168 | tf_op jit(solution)/shard_map/all_gather | solution.py:78
  629.7 8.8 %add_convert_fusion.1 = bf16[1024,512]{1,0:T(8,128)(2,1)} fusion(bf16[2048,512]{1,0:T(8,128)(2,1)} %all-gather.17.cloned.1.call-done, bf16[512,2048]{1,0:T(8,128)(2,1)} %reshape.1297, bf16[2,1,1024,512]{3,2,1,0:T(8,128)(2,1)} %param.15), kind=kOutput, calls=%fused_computation.126 | convolution fusion | flops 4315414528 | bytes 7340032 | tf_op jit(solution)/shard_map/bsf,fd->bsd/dot_general | solution.py:39
  638.5 57.1 %all-gather.19.cloned.1.call-done = bf16[2048,512]{1,0:T(8,128)(2,1)} async-done(((bf16[16,512]{1,0:T(8,128)(2,1)}), bf16[2048,512]{1,0:T(8,128)(2,1)}) %all-gather.19.cloned.1.call-update) | async-done | bytes 2097168 | tf_op jit(solution)/shard_map/all_gather | solution.py:78
  695.6 7.9 %fusion.147 = bf16[1,1,1024,512]{3,2,1,0:T(8,128)(2,1)} fusion(bf16[2048,512]{1,0:T(8,128)(2,1)} %all-gather.19.cloned.1.call-done, bf16[1024,512]{1,0:T(8,128)(2,1)} %add_convert_fusion.1, bf16[512,2048]{1,0:T(8,128)(2,1)S(1)} %reshape.1299), kind=kOutput, calls=%fused_computation.146 | convolution fusion | flops 4315414528 | bytes 6291456 | tf_op jit(solution)/shard_map/bsf,fd->bsd/dot_general | solution.py:39
  (108 shorter events, 149.1 us)
Async XLA Ops:
  31.9 11.3 %copy-start.17 = (bf16[1024,512]{1,0:T(8,128)(2,1)}, bf16[1024,512]{1,0:T(8,128)(2,1)S(1)}, u32[]{:S(2)}) copy-start(bf16[1024,512]{1,0:T(8,128)(2,1)S(1)} %add_convert_fusion.5) | copy-start | bytes 3145732
  45.4 42.7 %all-to-all-start = ((bf16[128,4,2048]{2,1,0:T(4,128)(2,1)}), bf16[128,4,2048]{2,1,0:T(4,128)(2,1)S(1)}, u32[]{:S(2)}, u32[]{:S(2)}) async-start(bf16[128,4,2048]{2,1,0:T(4,128)(2,1)} %all_to_all.48), calls=%async_computation | async-start | bytes 4194304 | tf_op jit(solution)/shard_map/all_to_all | solution.py:44
  89.5 40.1 %all-to-all-start.1 = ((bf16[128,4,2048]{2,1,0:T(4,128)(2,1)}), bf16[128,4,2048]{2,1,0:T(4,128)(2,1)S(1)}, u32[]{:S(2)}, u32[]{:S(2)}) async-start(bf16[128,4,2048]{2,1,0:T(4,128)(2,1)} %all_to_all.50), calls=%async_computation.1 | async-start | bytes 4194304 | tf_op jit(solution)/shard_map/all_to_all | solution.py:44
  123.6 16.5 %copy-start.6 = (f32[2,2,4,2048]{3,2,1,0:T(4,128)S(1)}, f32[2,2,4,2048]{3,2,1,0:T(4,128)}, u32[]{:S(2)}) copy-start(f32[2,2,4,2048]{3,2,1,0:T(4,128)} %param.20) | copy-start | bytes 393220
  123.6 16.5 %copy-start.7 = (f32[2,2,4,2048]{3,2,1,0:T(4,128)S(1)}, f32[2,2,4,2048]{3,2,1,0:T(4,128)}, u32[]{:S(2)}) copy-start(f32[2,2,4,2048]{3,2,1,0:T(4,128)} %param.18) | copy-start | bytes 393220
  123.6 16.5 %copy-start.8 = (f32[2,2,4,2048]{3,2,1,0:T(4,128)S(1)}, f32[2,2,4,2048]{3,2,1,0:T(4,128)}, u32[]{:S(2)}) copy-start(f32[2,2,4,2048]{3,2,1,0:T(4,128)} %param.22) | copy-start | bytes 393220
  123.6 16.5 %copy-start.9 = (f32[2,2,4,2048]{3,2,1,0:T(4,128)S(1)}, f32[2,2,4,2048]{3,2,1,0:T(4,128)}, u32[]{:S(2)}) copy-start(f32[2,2,4,2048]{3,2,1,0:T(4,128)} %param.24) | copy-start | bytes 393220
  129.6 41.3 %all-to-all-start.3 = ((bf16[128,4,2048]{2,1,0:T(4,128)(2,1)}), bf16[128,4,2048]{2,1,0:T(4,128)(2,1)}, u32[]{:S(2)}, u32[]{:S(2)}) async-start(bf16[128,4,2048]{2,1,0:T(4,128)(2,1)} %all_to_all.54), calls=%async_computation.3 | async-start | bytes 4194304 | tf_op jit(solution)/shard_map/all_to_all | solution.py:44
  140.0 251.1 %all-gather.21.cloned.1.call-start = ((), (), s32[]{:S(2)}) async-start(), calls=%async_computation.12 | async-start | bytes 2113536 | tf_op jit(solution)/shard_map/all_gather | solution.py:77
  171.0 39.3 %all-to-all-start.2 = ((bf16[128,4,2048]{2,1,0:T(4,128)(2,1)}), bf16[128,4,2048]{2,1,0:T(4,128)(2,1)}, u32[]{:S(2)}, u32[]{:S(2)}) async-start(bf16[128,4,2048]{2,1,0:T(4,128)(2,1)} %all_to_all.52), calls=%async_computation.2 | async-start | bytes 4194304 | tf_op jit(solution)/shard_map/all_to_all | solution.py:44
  177.3 217.7 %all-gather.23.cloned.1.call-start = ((), (), s32[]{:S(2)}) async-start(), calls=%async_computation.13 | async-start | bytes 2113536 | tf_op jit(solution)/shard_map/all_gather | solution.py:77
  213.6 185.4 %all-gather.27.cloned.1.call-start = ((), (), s32[]{:S(2)}) async-start(), calls=%async_computation.15 | async-start | bytes 2113536 | tf_op jit(solution)/shard_map/all_gather | solution.py:77
  222.9 36.8 %all-to-all-start.5 = ((bf16[128,16,512]{2,1,0:T(8,128)(2,1)}), bf16[128,16,512]{2,1,0:T(8,128)(2,1)S(1)}, u32[]{:S(2)}, u32[]{:S(2)}) async-start(bf16[128,16,512]{2,1,0:T(8,128)(2,1)} %bitcast.742), calls=%async_computation.5 | async-start | bytes 4194304 | tf_op jit(solution)/shard_map/all_to_all | solution.py:44
  259.7 38.3 %all-to-all-start.4 = ((bf16[128,16,512]{2,1,0:T(8,128)(2,1)}), bf16[128,16,512]{2,1,0:T(8,128)(2,1)}, u32[]{:S(2)}, u32[]{:S(2)}) async-start(bf16[128,16,512]{2,1,0:T(8,128)(2,1)} %bitcast.740), calls=%async_computation.4 | async-start | bytes 4194304 | tf_op jit(solution)/shard_map/all_to_all | solution.py:44
  266.0 166.3 %all-gather.25.cloned.1.call-start = ((), (), s32[]{:S(2)}) async-start(), calls=%async_computation.14 | async-start | bytes 2113536 | tf_op jit(solution)/shard_map/all_gather | solution.py:77
  275.1 66.3 %copy-start.2 = (f32[2,2,16,512]{3,2,1,0:T(8,128)S(1)}, f32[2,2,16,512]{3,2,1,0:T(8,128)}, u32[]{:S(2)}) copy-start(f32[2,2,16,512]{3,2,1,0:T(8,128)} %param.21) | copy-start | bytes 393220
  275.1 66.3 %copy-start.3 = (f32[2,2,16,512]{3,2,1,0:T(8,128)S(1)}, f32[2,2,16,512]{3,2,1,0:T(8,128)}, u32[]{:S(2)}) copy-start(f32[2,2,16,512]{3,2,1,0:T(8,128)} %param.19) | copy-start | bytes 393220
  275.1 66.3 %copy-start.4 = (f32[2,2,16,512]{3,2,1,0:T(8,128)S(1)}, f32[2,2,16,512]{3,2,1,0:T(8,128)}, u32[]{:S(2)}) copy-start(f32[2,2,16,512]{3,2,1,0:T(8,128)} %param.23) | copy-start | bytes 393220
  275.1 66.3 %copy-start.5 = (f32[2,2,16,512]{3,2,1,0:T(8,128)S(1)}, f32[2,2,16,512]{3,2,1,0:T(8,128)}, u32[]{:S(2)}) copy-start(f32[2,2,16,512]{3,2,1,0:T(8,128)} %param.25) | copy-start | bytes 393220
  298.0 41.4 %all-to-all-start.6 = ((bf16[128,16,512]{2,1,0:T(8,128)(2,1)}), bf16[128,16,512]{2,1,0:T(8,128)(2,1)}, u32[]{:S(2)}, u32[]{:S(2)}) async-start(bf16[128,16,512]{2,1,0:T(8,128)(2,1)} %bitcast.741), calls=%async_computation.6 | async-start | bytes 4194304 | tf_op jit(solution)/shard_map/all_to_all | solution.py:44
  304.3 193.7 %all-gather.13.cloned.1.call-start = ((), (), s32[]{:S(2)}) async-start(), calls=%async_computation.8 | async-start | bytes 2113536 | tf_op jit(solution)/shard_map/all_gather | solution.py:78
  342.1 221.7 %all-gather.15.cloned.1.call-start = ((), (), s32[]{:S(2)}) async-start(), calls=%async_computation.9 | async-start | bytes 2113536 | tf_op jit(solution)/shard_map/all_gather | solution.py:78
  342.7 287.0 %all-gather.17.cloned.1.call-start = ((), (), s32[]{:S(2)}) async-start(), calls=%async_computation.10 | async-start | bytes 2113536 | tf_op jit(solution)/shard_map/all_gather | solution.py:78
  343.5 352.2 %all-gather.19.cloned.1.call-start = ((), (), s32[]{:S(2)}) async-start(), calls=%async_computation.11 | async-start | bytes 2113536 | tf_op jit(solution)/shard_map/all_gather | solution.py:78
  (9 other events, 46.2 us)
Sparse Core Ops, SparseCore 0:
  144.0 71.0 all-gather.20
  218.1 70.4 all-gather.22
  291.8 70.9 all-gather.26
  365.8 66.4 all-gather.24
  435.3 62.7 all-gather.12
  501.0 62.7 all-gather.14
  566.9 62.7 all-gather.16
  632.9 62.7 all-gather.18
where the time goes:
time: 716 us; the launch traced here: 713 us
  waiting for transfers between devices  402 us (56%)
  matrix products  153 us (21%)
  starting transfers between devices  52.8 us (7%)
  blocking collectives  34.7 us (5%)
  local copies, waits for them, and re-layouts  34.6 us (5%)
  other arithmetic  21.5 us (3%)
  between operations  14.7 us (2%)
    all_gather x4, waiting for transfers between devices, device_step(): lax.all_gather(new_down[0].astype(jnp.bfloat16), 'fsdp', axis=0, tiled=True)  234 us
    all_to_all x7, waiting for transfers between devices, scatter_sum(): lax.all_to_all(part.astype(jnp.bfloat16), 'fsdp', 0, 0, tiled=True)  134 us
    all_to_all x7, starting transfers between devices, scatter_sum(): lax.all_to_all(part.astype(jnp.bfloat16), 'fsdp', 0, 0, tiled=True)  52.4 us
    dot_general x4, matrix products, backward_layer(): jnp.einsum('bsd,bsf->df', x_in, grad_hidden, preferred_element_type=jnp.f...  35.1 us
    all_to_all x1, blocking collectives, scatter_sum(): lax.all_to_all(part.astype(jnp.bfloat16), 'fsdp', 0, 0, tiled=True)  34.7 us
    dot_general x4, matrix products, backward_layer(): jnp.einsum('bsf,bsd->fd', gelu_out.astype(jnp.bfloat16), cotangent, prefe...  32.9 us
    dot_general x4, matrix products, forward_layer(): jnp.einsum('bsf,fd->bsd', gelu_out, w_two, preferred_element_type=jnp.flo...  32.8 us
    all_gather x4, waiting for transfers between devices, device_step(): lax.all_gather(new_up[0].astype(jnp.bfloat16), 'fsdp', axis=0, tiled=True)  30.7 us
  transfers between devices with their start and end apart: 15, of which 11 were waited for; matrix products, arithmetic and copies ran while one was open for 20% of the time, Pallas kernels for 0%

commit v1 on v0

v1 whole, which is shorter than its diff:
```python
import functools
import jax
import jax.numpy as jnp
from jax import lax
from jax.experimental import pallas as pl
from jax.experimental.pallas import tpu as pltpu
from jax.sharding import PartitionSpec as P

LEARN_RATE = 0.005
BETA_ONE = 0.9
BETA_TWO = 0.95
ADAM_EPS = 1e-8
WEIGHT_DECAY = 0.1
MICROBATCHES = 2
ADAM_STEP = 2
MESH = pl.DeviceIdType.MESH

ORDERS = ((2, 1, 0), (1, 0, 2), (0, 2, 1))
RS_LANES = ((0, 768), (768, 640), (1408, 640))
AG_LANES = ((0, 384), (384, 384), (768, 256))
TASKS = ((0, 1), (0, 0), (1, 1), (1, 0))
PHASES = 13
STAGGER = 2


def adam_update(acc_part, grad_new, master, moment_one, moment_two):
    grad_mean = (acc_part + grad_new) / MICROBATCHES
    moment_one = BETA_ONE * moment_one + (1.0 - BETA_ONE) * grad_mean
    moment_two = BETA_TWO * moment_two + (1.0 - BETA_TWO) * grad_mean * grad_mean
    corr_one = 1.0 - BETA_ONE ** ADAM_STEP
    corr_two = 1.0 - BETA_TWO ** ADAM_STEP
    step_dir = (moment_one / corr_one) / (jnp.sqrt(moment_two / corr_two) + ADAM_EPS)
    master = master - LEARN_RATE * (step_dir + WEIGHT_DECAY * master)
    return master, moment_one, moment_two


def backward_layer(x_in, cotangent, w_one, w_two):
    hidden = jnp.einsum('bsd,df->bsf', x_in, w_one, preferred_element_type=jnp.float32)
    gelu_out, gelu_vjp = jax.vjp(jax.nn.gelu, hidden)
    grad_act = jnp.einsum('bsd,fd->bsf', cotangent, w_two, preferred_element_type=jnp.float32)
    grad_hidden = gelu_vjp(grad_act)[0].astype(jnp.bfloat16)
    part_down = jnp.einsum('bsf,bsd->fd', gelu_out.astype(jnp.bfloat16), cotangent, preferred_element_type=jnp.float32)
    part_up = jnp.einsum('bsd,bsf->df', x_in, grad_hidden, preferred_element_type=jnp.float32)
    return part_up.astype(jnp.bfloat16), part_down.astype(jnp.bfloat16), grad_hidden


def forward_layer(x_in, w_one, w_two):
    hidden = jnp.einsum('bsd,df->bsf', x_in, w_one, preferred_element_type=jnp.float32)
    gelu_out = jax.nn.gelu(hidden).astype(jnp.bfloat16)
    mlp_val = jnp.einsum('bsf,fd->bsd', gelu_out, w_two, preferred_element_type=jnp.float32)
    return (x_in.astype(jnp.float32) + mlp_val).astype(jnp.bfloat16)


def half_dim(axis):
    return 1 if axis == 0 else 0


def region(fixed, lanes):
    return tuple(fixed.get(dim, slice(None)) for dim in range(3)) + (slice(None), pl.ds(lanes[0], lanes[1]))


def comm_kernel(*refs):
    ups, downs = refs[0:4], refs[4:8]
    acc_up, acc_down, master_up, master_down, m1_up, m1_down, m2_up, m2_down = refs[8:16]
    out_states = refs[16:22]
    gath_out = refs[22]
    (own_up, own_down, recv_up, recv_down, plane, rs1, rs2, rs3, rs4, grad_x, part_x, block8, gath, local_sem, send_sem, recv_sem) = refs[23:]

    me = lax.axis_index('fsdp')
    core = lax.rem(me, 2)
    chip = lax.div(me, 2)
    pos = (lax.div(chip, 16), lax.rem(lax.div(chip, 4), 4), lax.rem(chip, 4))
    stride = (32, 8, 2)
    partner = me + 1 - 2 * core

    def at_axis(axis, step):
        return lax.rem(pos[axis] + step, 4)

    def peer(axis, step):
        return me + (at_axis(axis, step) - pos[axis]) * stride[axis]

    barrier = pltpu.get_barrier_semaphore()
    pl.semaphore_signal(barrier, inc=1, device_id=(partner,), device_id_type=MESH)
    for axis in range(3):
        for step in (1, 2, 3):
            pl.semaphore_signal(barrier, inc=1, device_id=(peer(axis, step),), device_id_type=MESH)
    pl.semaphore_wait(barrier, 10)

    class Task:
        def __init__(self, task_id):
            self.t = task_id
            self.par = task_id % 2
            self.slot = 0
            self.live = []
            self.stage, self.layer = TASKS[task_id]

        def send(self, src, dst, device):
            copy = pltpu.make_async_remote_copy(src_ref=src, dst_ref=dst, send_sem=send_sem.at[self.t, self.slot], recv_sem=recv_sem.at[self.t, self.slot], device_id=(device,), device_id_type=MESH)
            self.slot += 1
            copy.start()
            self.live.append(copy)

        def drain(self):
            for copy in self.live:
                copy.wait()
            self.live = []

        def plane_at(self, fixed, g):
            return plane.at[(self.par,) + region(fixed, RS_LANES[g])]

        def gath_at(self, fixed, g):
            return gath.at[(self.t, core) + region(fixed, AG_LANES[g])]

        def run(self, phase):
            getattr(self, 'phase_%d' % phase)()

        def phase_0(self):
            t, par = self.t, self.par
            self.send(ups[t].at[:, pl.ds(pl.multiple_of((1 - core) * 1024, 1024), 1024)], recv_up.at[t], partner)
            self.send(downs[t].at[:, 1 - core], recv_down.at[t], partner)
            first = pltpu.make_async_copy(ups[t].at[:, pl.ds(pl.multiple_of(core * 1024, 1024), 1024)], own_up.at[par], local_sem.at[t, 0])
            second = pltpu.make_async_copy(downs[t].at[:, core], own_down.at[par], local_sem.at[t, 1])
            first.start()
            second.start()
            self.local = [first, second]

        def phase_1(self):
            t, par = self.t, self.par
            for copy in self.local:
                copy.wait()
            self.drain()

            def body(i, carry):
                z_pos, y_pos = lax.div(i, 4), lax.rem(i, 4)
                rows = pl.ds(pl.multiple_of(i * 32, 32), 32)
                up_sum = own_up[par, rows, :].astype(jnp.float32) + recv_up[t, rows, :].astype(jnp.float32)
                plane[par, z_pos, y_pos, :, :, 0:1024] = up_sum.reshape(4, 8, 1024)
                chips = pl.ds(i * 4, 4)
                down_sum = own_down[par, chips].astype(jnp.float32) + recv_down[t, chips].astype(jnp.float32)
                plane[par, z_pos, y_pos, :, :, 1024:1536] = down_sum[:, 0:8, :]
                plane[par, z_pos, y_pos, :, :, 1536:2048] = down_sum[:, 8:16, :]
                return carry

            lax.fori_loop(0, 16, body, 0)
            for g, order in enumerate(ORDERS):
                axis, half = order[0], half_dim(order[0])
                lanes = pl.ds(*RS_LANES[g])
                far = at_axis(axis, 2)
                self.send(self.plane_at({axis: far, half: pl.ds(0, 2)}, g), rs1.at[t, 0, :, :, :, lanes], peer(axis, 1))
                self.send(self.plane_at({axis: far, half: pl.ds(2, 2)}, g), rs1.at[t, 1, :, :, :, lanes], peer(axis, 3))

        def phase_2(self):
            t, par = self.t, self.par
            self.drain()
            for g, order in enumerate(ORDERS):
                axis, half = order[0], half_dim(order[0])
                lanes = pl.ds(*RS_LANES[g])
                for way, step in ((0, 1), (1, 3)):
                    dest = at_axis(axis, step)
                    where = (par,) + region({axis: dest, half: pl.ds(2 * way, 2)}, RS_LANES[g])
                    plane[where] = plane[where] + rs1[t, way, :, :, :, lanes]
                    self.send(self.plane_at({axis: dest}, g), rs2.at[t, way, :, :, :, lanes], peer(axis, step))

        def phase_3(self):
            t, par = self.t, self.par
            self.drain()
            for g, order in enumerate(ORDERS):
                lanes = pl.ds(*RS_LANES[g])
                where = (par,) + region({order[0]: pos[order[0]]}, RS_LANES[g])
                plane[where] = plane[where] + (rs2[t, 0, :, :, :, lanes] + rs2[t, 1, :, :, :, lanes])
                for step in (1, 2, 3):
                    self.send(self.plane_at({order[0]: pos[order[0]], order[1]: at_axis(order[1], step)}, g), rs3.at[t, step - 1, :, :, lanes], peer(order[1], step))

        def phase_4(self):
            t, par = self.t, self.par
            self.drain()
            for g, order in enumerate(ORDERS):
                lanes = pl.ds(*RS_LANES[g])
                fixed = {order[0]: pos[order[0]], order[1]: pos[order[1]]}
                where = (par,) + region(fixed, RS_LANES[g])
                plane[where] = plane[where] + (rs3[t, 0, :, :, lanes] + rs3[t, 1, :, :, lanes] + rs3[t, 2, :, :, lanes])
                for step in (1, 2, 3):
                    self.send(self.plane_at({**fixed, order[2]: at_axis(order[2], step)}, g), rs4.at[t, step - 1, :, lanes], peer(order[2], step))

        def phase_5(self):
            t, par = self.t, self.par
            self.drain()
            block = plane[par, pos[0], pos[1], pos[2]] + (rs4[t, 0] + rs4[t, 1] + rs4[t, 2])
            block8[t] = block
            grad_x[t, core] = block[:, 0:1024]
            self.send(grad_x.at[t, core], grad_x.at[t, core], partner)

        def phase_6(self):
            t, s, l = self.t, self.stage, self.layer
            self.drain()
            grad_down = jnp.concatenate([block8[t, :, 1024:1536], block8[t, :, 1536:2048]], axis=0)
            new_down = adam_update(acc_down[s, l], grad_down, master_down[s, l], m1_down[s, l], m2_down[s, l])
            low = jnp.concatenate([grad_x[t, 0, 0:4, :], grad_x[t, 1, 0:4, :]], axis=1)
            high = jnp.concatenate([grad_x[t, 0, 4:8, :], grad_x[t, 1, 4:8, :]], axis=1)
            grad_up = jnp.where(core == 0, low, high)
            new_up = adam_update(acc_up[s, l], grad_up, master_up[s, l], m1_up[s, l], m2_up[s, l])
            for i in range(3):
                out_states[2 * i][s, l] = new_up[i]
                out_states[2 * i + 1][s, l] = new_down[i]
            left, right = new_up[0][:, 0:1024], new_up[0][:, 1024:2048]
            part_x[t, core] = jnp.where(core == 0, left, right)
            part_x[t, 2] = jnp.where(core == 0, right, left)
            self.send(part_x.at[t, 2], part_x.at[t, core], partner)
            gath[t, core, pos[0], pos[1], pos[2], :, 512:1024] = new_down[0].astype(jnp.bfloat16)

        def phase_7(self):
            t = self.t
            self.drain()
            block8[t, 0:4, 0:1024] = part_x[t, 0]
            block8[t, 4:8, 0:1024] = part_x[t, 1]
            rows = jnp.concatenate([block8[t, :, 0:512], block8[t, :, 512:1024]], axis=0)
            gath[t, core, pos[0], pos[1], pos[2], :, 0:512] = rows.astype(jnp.bfloat16)
            for g, order in enumerate(ORDERS):
                where = self.gath_at({0: pos[0], 1: pos[1], 2: pos[2]}, g)
                for step in (1, 2, 3):
                    self.send(where, where, peer(order[2], step))

        def phase_8(self):
            self.drain()
            for g, order in enumerate(ORDERS):
                where = self.gath_at({order[0]: pos[order[0]], order[1]: pos[order[1]]}, g)
                for step in (1, 2, 3):
                    self.send(where, where, peer(order[1], step))

        def phase_9(self):
            self.drain()
            for g, order in enumerate(ORDERS):
                where = self.gath_at({order[0]: pos[order[0]]}, g)
                for step in (1, 3):
                    self.send(where, where, peer(order[0], step))

        def phase_10(self):
            self.drain()
            for g, order in enumerate(ORDERS):
                axis, half = order[0], half_dim(order[0])
                for way, step in ((0, 1), (1, 3)):
                    where = self.gath_at({axis: at_axis(axis, 4 - step), half: pl.ds(2 * way, 2)}, g)
                    self.send(where, where, peer(axis, step))

        def phase_11(self):
            self.drain()
            self.send(gath.at[self.t, core], gath.at[self.t, core], partner)

        def phase_12(self):
            self.drain()
            copy = pltpu.make_async_copy(gath.at[self.t], gath_out.at[self.t], local_sem.at[self.t, 2])
            copy.start()
            self.local = [copy]

    tasks = [Task(t) for t in range(4)]
    for tick in range(PHASES + 3 * STAGGER):
        for t in range(4):
            phase = tick - STAGGER * t
            if 0 <= phase < PHASES:
                tasks[t].run(phase)
    for task in tasks:
        for copy in task.local:
            copy.wait()


def communicate(ups, downs, states):
    vmem = pl.BlockSpec(memory_space=pltpu.VMEM)
    hbm = pl.BlockSpec(memory_space=pl.ANY)
    up_state = jax.ShapeDtypeStruct(states[0].shape, jnp.float32)
    down_state = jax.ShapeDtypeStruct(states[1].shape, jnp.float32)
    scratch = [
        pltpu.VMEM((2, 512, 1024), jnp.bfloat16),
        pltpu.VMEM((2, 64, 16, 512), jnp.bfloat16),
        pltpu.VMEM((4, 512, 1024), jnp.bfloat16),
        pltpu.VMEM((4, 64, 16, 512), jnp.bfloat16),
        pltpu.VMEM((2, 4, 4, 4, 8, 2048), jnp.float32),
        pltpu.VMEM((4, 2, 2, 4, 8, 2048), jnp.float32),
        pltpu.VMEM((4, 2, 4, 4, 8, 2048), jnp.float32),
        pltpu.VMEM((4, 3, 4, 8, 2048), jnp.float32),
        pltpu.VMEM((4, 3, 8, 2048), jnp.float32),
        pltpu.VMEM((4, 2, 8, 1024), jnp.float32),
        pltpu.VMEM((4, 3, 4, 1024), jnp.float32),
        pltpu.VMEM((4, 8, 2048), jnp.float32),
        pltpu.VMEM((4, 2, 4, 4, 4, 16, 1024), jnp.bfloat16),
        pltpu.SemaphoreType.DMA((4, 3)),
        pltpu.SemaphoreType.DMA((4, 66)),
        pltpu.SemaphoreType.DMA((4, 66)),
    ]
    return pl.pallas_call(
        comm_kernel,
        out_shape=(up_state, down_state) * 3 + (jax.ShapeDtypeStruct((4, 2, 4, 4, 4, 16, 1024), jnp.bfloat16),),
        in_specs=[hbm] * 8 + [vmem] * 8,
        out_specs=(vmem,) * 6 + (hbm,),
        scratch_shapes=scratch,
        compiler_params=pltpu.CompilerParams(collective_id=0, has_side_effects=True, vmem_limit_bytes=67043328),
        name='exchange',
    )(*ups, *downs, *states)


def solution(mesh):
    tok_spec = P(None, 'fsdp')
    layer_spec = P(None, None, 'fsdp')
    rep_spec = P()

    def device_step(x_saved, grad_out, x_next, w_up, w_down, acc_up, acc_down, master_up, master_down, moment1_up, moment1_down, moment2_up, moment2_down):
        ups, downs = [], []
        for stage_id in range(2):
            cotangent = grad_out[stage_id]
            for layer_id in (1, 0):
                cur_up = w_up[stage_id, layer_id]
                part_up, part_down, grad_hidden = backward_layer(x_saved[stage_id, layer_id], cotangent, cur_up, w_down[stage_id, layer_id])
                if layer_id > 0:
                    cotangent = (cotangent.astype(jnp.float32) + jnp.einsum('bsf,df->bsd', grad_hidden, cur_up, preferred_element_type=jnp.float32)).astype(jnp.bfloat16)
                ups.append(part_up)
                downs.append(part_down.reshape(64, 2, 16, 512))
        result = communicate(ups, downs, (acc_up, acc_down, master_up, master_down, moment1_up, moment1_down, moment2_up, moment2_down))
        gath = result[6].reshape(4, 2, 64, 16, 1024)
        y_list = []
        for stage_id in range(2):
            hidden_x = x_next[stage_id]
            for layer_id in range(2):
                part = gath[TASKS.index((stage_id, layer_id))]
                full_down = part[:, :, :, 512:].transpose(1, 0, 2, 3).reshape(2048, 512)
                full_up = part[:, :, :, :512].reshape(2, 64, 2, 8, 512).transpose(1, 3, 0, 2, 4).reshape(512, 2048)
                hidden_x = forward_layer(hidden_x, full_up, full_down)
            y_list.append(hidden_x)
        return result[:6] + (jnp.stack(y_list),)

    return jax.shard_map(device_step, mesh=mesh, in_specs=(layer_spec, tok_spec, tok_spec, rep_spec, rep_spec) + (layer_spec,) * 8, out_specs=(layer_spec,) * 6 + (tok_spec,), check_vma=False)
```

time: 716 us -> 349 us (0.49)
  waiting for transfers between devices: 402 us -> 0 us
  Pallas kernels: 0 us -> 155 us
  starting transfers between devices: 52.8 us -> 0 us
  blocking collectives: 34.7 us -> 0 us
  matrix products: 153 us -> 125 us
  local copies, waits for them, and re-layouts: 34.6 us -> 62.3 us
  other arithmetic: 21.5 us -> 2.73 us
  between operations: 14.7 us -> 1.13 us
    all_gather x8 -> x0, waiting for transfers between devices: 265 us -> none  [the longest x4 234 us: device_step(): lax.all_gather(new_down[0].astype(jnp.bfloat16), 'fsdp', axis=0, tiled=True)]
    pallas_call x0 -> x1, Pallas kernels: none -> 155 us  [communicate(): pl.pallas_call(comm_kernel, out_shape=(up_state, down_state) * 3 + (jax.S...]
    all_to_all x7 -> x0, waiting for transfers between devices: 134 us -> none  [scatter_sum(): lax.all_to_all(part.astype(jnp.bfloat16), 'fsdp', 0, 0, tiled=True)]
    all_to_all x7 -> x0, starting transfers between devices: 52.4 us -> none  [scatter_sum(): lax.all_to_all(part.astype(jnp.bfloat16), 'fsdp', 0, 0, tiled=True)]
    all_to_all x1 -> x0, blocking collectives: 34.7 us -> none  [scatter_sum(): lax.all_to_all(part.astype(jnp.bfloat16), 'fsdp', 0, 0, tiled=True)]
    transpose x0 -> x12, local copies, waits for them, and re-layouts: none -> 32.2 us  [the longest x8 22.4 us: device_step(): part[:, :, :, :512].reshape(2, 64, 2, 8, 512).transpose(1, 3, 0, 2, 4)]
    dot_general x4, matrix products: 32.9 us -> 18.1 us  [backward_layer(): jnp.einsum('bsf,bsd->fd', gelu_out.astype(jnp.bfloat16), cotangent, prefe...]
    all_to_all x4 -> x0, local copies, waits for them, and re-layouts: 14.7 us -> none  [scatter_sum(): lax.all_to_all(part.astype(jnp.bfloat16), 'fsdp', 0, 0, tiled=True)]
  transfers between devices with their start and end apart: 15 -> 0, of which waited for: 11 -> 0; matrix products, arithmetic and copies ran while one was open for 20% -> 0% of each run, Pallas kernels for 0% -> 0%
where the time goes in v1:
time: 349 us; the launch traced here: 346 us
  Pallas kernels  155 us (44%)
  matrix products  125 us (36%)
  local copies, waits for them, and re-layouts  62.3 us (18%)
    pallas_call x1, Pallas kernels, communicate(): pl.pallas_call(comm_kernel, out_shape=(up_state, down_state) * 3 + (jax.S...  155 us
    dot_general x4, matrix products, backward_layer(): jnp.einsum('bsd,bsf->df', x_in, grad_hidden, preferred_element_type=jnp.f...  33.3 us
    dot_general x4, matrix products, forward_layer(): jnp.einsum('bsf,fd->bsd', gelu_out, w_two, preferred_element_type=jnp.flo...  32.4 us
    transpose x8, local copies, waits for them, and re-layouts, device_step(): part[:, :, :, :512].reshape(2, 64, 2, 8, 512).transpose(1, 3, 0, 2, 4)  22.4 us
    dot_general x4, matrix products, backward_layer(): jnp.einsum('bsd,df->bsf', x_in, w_one, preferred_element_type=jnp.float32)  18.8 us
    dot_general x4, matrix products, backward_layer(): jnp.einsum('bsf,bsd->fd', gelu_out.astype(jnp.bfloat16), cotangent, prefe...  18.1 us
    dot_general x2, matrix products, backward_layer(): jnp.einsum('bsd,fd->bsf', cotangent, w_two, preferred_element_type=jnp.fl...  16.1 us
    reshape x4, local copies, waits for them, and re-layouts, device_step(): part[:, :, :, :512].reshape(2, 64, 2, 8, 512).transpose(1, 3, 0, 2, 4)  11.9 us

profile of v1, /device:TPU:1, one launch (start us, length us, event | category | flops | bytes accessed | tf_op | source)
XLA Modules:
  0.0 345.8 jit_solution(6573345513722335833)
XLA Ops:
  0.6 4.4 %fusion.106 = f32[1024,2048]{1,0:T(8,128)S(1)} fusion(bf16[2,2,512,2048]{3,2,1,0:T(8,128)(2,1)} %param.16, bf16[2,2,1,1024,512]{4,3,2,1,0:T(8,128)(2,1)} %param.13), kind=kOutput, calls=%fused_computation.116 | convolution fusion | flops 2147483648 | bytes 11534336 | tf_op jit(solution)/shard_map/bsd,df->bsf/dot_general | solution.py:38
  5.1 4.5 %fusion.112 = f32[1024,2048]{1,0:T(8,128)S(1)} fusion(bf16[2,2,512,2048]{3,2,1,0:T(8,128)(2,1)S(1)} %copy-done.5, bf16[2,2,1,1024,512]{4,3,2,1,0:T(8,128)(2,1)} %param.13), kind=kOutput, calls=%fused_computation.121 | convolution fusion | flops 2147483648 | bytes 11534336 | tf_op jit(solution)/shard_map/bsd,df->bsf/dot_general | solution.py:38
  9.6 4.9 %fusion.79 = bf16[2048,512]{1,0:T(8,128)(2,1)} fusion(f32[1024,2048]{1,0:T(8,128)S(1)} %fusion.112, bf16[2,1,1024,512]{3,2,1,0:T(8,128)(2,1)S(1)} %copy-done.7), kind=kOutput, calls=%fused_computation.91 | convolution fusion | flops 2167406592 | bytes 11534336 | tf_op jit(solution)/shard_map/bsf,bsd->fd/dot_general | solution.py:42
  14.5 8.0 %fusion.6 = bf16[1024,2048]{1,0:T(8,128)(2,1)S(1)} fusion(f32[1024,2048]{1,0:T(8,128)S(1)} %fusion.112, bf16[2,2,2048,512]{3,2,1,0:T(8,128)(2,1)} %param.17, bf16[2,1,1024,512]{3,2,1,0:T(8,128)(2,1)S(1)} %copy-done.7), kind=kOutput, calls=%fused_computation.18 | convolution fusion | flops 2189426688 | bytes 15728640 | tf_op jit(solution)/shard_map/bsd,fd->bsf/dot_general | solution.py:40
  24.9 5.1 %fusion.92.refs_0_ = bf16[512,2048]{1,0:T(8,128)(2,1)} fusion(bf16[1024,2048]{1,0:T(8,128)(2,1)S(1)} %fusion.6, bf16[2,2,1,1024,512]{4,3,2,1,0:T(8,128)(2,1)} %param.13), kind=kOutput, calls=%fused_computation.96 | convolution fusion | flops 2148532224 | bytes 7340032 | tf_op jit(solution)/shard_map/bsd,bsf->df/dot_general | solution.py:43
  30.0 4.4 %fusion.78 = bf16[2048,512]{1,0:T(8,128)(2,1)} fusion(bf16[1024,512]{1,0:T(8,128)(2,1)S(1)} %add_convert_fusion.5, f32[1024,2048]{1,0:T(8,128)S(1)} %fusion.106), kind=kOutput, calls=%fused_computation.90 | convolution fusion | flops 2167406592 | bytes 11534336 | tf_op jit(solution)/shard_map/bsf,bsd->fd/dot_general | solution.py:42
  34.3 12.1 %fusion.89.refs_1_ = bf16[512,2048]{1,0:T(8,128)(2,1)} fusion(f32[1024,2048]{1,0:T(8,128)} %copy-done.8, bf16[1024,512]{1,0:T(8,128)(2,1)S(1)} %add_convert_fusion.5, bf16[2,2,2048,512]{3,2,1,0:T(8,128)(2,1)} %param.17, bf16[2,2,1,1024,512]{4,3,2,1,0:T(8,128)(2,1)} %param.13), kind=kOutput, calls=%fused_computation.95 | convolution fusion | flops 4337958912 | bytes 14680064 | tf_op jit(solution)/shard_map/bsd,bsf->df/dot_general | solution.py:43
  46.4 4.4 %fusion.94 = f32[1024,2048]{1,0:T(8,128)S(1)} fusion(bf16[2,2,512,2048]{3,2,1,0:T(8,128)(2,1)} %param.16, bf16[2,2,1,1024,512]{4,3,2,1,0:T(8,128)(2,1)} %param.13), kind=kOutput, calls=%fused_computation.107 | convolution fusion | flops 2147483648 | bytes 11534336 | tf_op jit(solution)/shard_map/bsd,df->bsf/dot_general | solution.py:38
  50.8 5.5 %fusion.100 = f32[1024,2048]{1,0:T(8,128)S(1)} fusion(bf16[2,2,512,2048]{3,2,1,0:T(8,128)(2,1)} %param.16, bf16[2,2,1,1024,512]{4,3,2,1,0:T(8,128)(2,1)S(1)} %copy-done.6), kind=kOutput, calls=%fused_computation.112 | convolution fusion | flops 2147483648 | bytes 11534336 | tf_op jit(solution)/shard_map/bsd,df->bsf/dot_general | solution.py:38
  56.3 4.4 %fusion.77 = bf16[2048,512]{1,0:T(8,128)(2,1)} fusion(f32[1024,2048]{1,0:T(8,128)S(1)} %fusion.100, bf16[2,1,1024,512]{3,2,1,0:T(8,128)(2,1)S(1)} %copy-done.7), kind=kOutput, calls=%fused_computation.89 | convolution fusion | flops 2167406592 | bytes 11534336 | tf_op jit(solution)/shard_map/bsf,bsd->fd/dot_general | solution.py:42
  60.7 8.2 %fusion.20 = bf16[1024,2048]{1,0:T(8,128)(2,1)S(1)} fusion(f32[1024,2048]{1,0:T(8,128)S(1)} %fusion.100, bf16[2,2,2048,512]{3,2,1,0:T(8,128)(2,1)} %param.17, bf16[2,1,1024,512]{3,2,1,0:T(8,128)(2,1)S(1)} %copy-done.7), kind=kOutput, calls=%fused_computation.32 | convolution fusion | flops 2189426688 | bytes 15728640 | tf_op jit(solution)/shard_map/bsd,fd->bsf/dot_general | solution.py:40
  68.9 4.0 %add_convert_fusion.4 = bf16[1024,512]{1,0:T(8,128)(2,1)S(1)} fusion(bf16[1024,2048]{1,0:T(8,128)(2,1)S(1)} %fusion.20, bf16[2,2,512,2048]{3,2,1,0:T(8,128)(2,1)} %param.16, bf16[2,1,1024,512]{3,2,1,0:T(8,128)(2,1)S(1)} %copy-done.7), kind=kOutput, calls=%fused_computation.131 | convolution fusion | flops 2149056512 | bytes 8388608 | tf_op jit(solution)/shard_map/bsf,df->bsd/dot_general | solution.py:313
  72.9 3.8 %fusion.93.refs_2_ = bf16[512,2048]{1,0:T(8,128)(2,1)} fusion(bf16[1024,2048]{1,0:T(8,128)(2,1)S(1)} %fusion.20, bf16[2,2,1,1024,512]{4,3,2,1,0:T(8,128)(2,1)S(1)} %copy-done.6), kind=kOutput, calls=%fused_computation.97 | convolution fusion | flops 2148532224 | bytes 7340032 | tf_op jit(solution)/shard_map/bsd,bsf->df/dot_general | solution.py:43
  76.7 4.4 %fusion.76 = bf16[2048,512]{1,0:T(8,128)(2,1)} fusion(bf16[1024,512]{1,0:T(8,128)(2,1)S(1)} %add_convert_fusion.4, f32[1024,2048]{1,0:T(8,128)S(1)} %fusion.94), kind=kOutput, calls=%fused_computation.88 | convolution fusion | flops 2167406592 | bytes 11534336 | tf_op jit(solution)/shard_map/bsf,bsd->fd/dot_general | solution.py:42
  81.1 12.4 %fusion.86.refs_3_ = bf16[512,2048]{1,0:T(8,128)(2,1)} fusion(f32[1024,2048]{1,0:T(8,128)} %copy-done.9, bf16[1024,512]{1,0:T(8,128)(2,1)S(1)} %add_convert_fusion.4, bf16[2,2,2048,512]{3,2,1,0:T(8,128)(2,1)} %param.17, bf16[2,2,1,1024,512]{4,3,2,1,0:T(8,128)(2,1)} %param.13), kind=kOutput, calls=%fused_computation.94 | convolution fusion | flops 4337958912 | bytes 14680064 | tf_op jit(solution)/shard_map/bsd,bsf->df/dot_general | solution.py:43
  93.5 154.6 %exchange.1 = (f32[2,2,4,2048]{3,2,1,0:T(4,128)}, f32[2,2,16,512]{3,2,1,0:T(8,128)}, f32[2,2,4,2048]{3,2,1,0:T(4,128)}, f32[2,2,16,512]{3,2,1,0:T(8,128)}, f32[2...) custom-call(bf16[512,2048]{1,0:T(8,128)(2,1)} %fusion.92.refs_0_, ...), custom_call_target="tpu_custom_call" | custom-call | tf_op jit(solution)/shard_map/exchange/pallas_call | solution.py:289
  248.1 11.5 %fusion.226 = (bf16[1,2,4,4,4,16,1024]{6,5,4,3,2,1,0:T(8,128)(2,1)}, bf16[1,2,4,4,4,16,1024]{6,5,4,3,2,1,0:T(8,128)(2,1)S(1)}, bf16[1,2,4,4,4,16,1024]{6,5,4,3,2...) fusion(bf16[4,2,4,4,4,16,1024]{6,5,4,3,2,1,0:T(8,128)(2,1)} %get-tuple-element.20), kind=kLoop, calls=%fused_computation.219 | loop fusion | bytes 33554432 | tf_op jit(solution)/shard_map/slice | solution.py:322
  266.5 4.0 %slice_bitcast_fusion.7 = (bf16[64,8,2,2,512]{4,1,3,0,2:T(8,128)(2,1)S(1)}, bf16[64,2,16,512]{3,2,0,1:T(8,128)(2,1)}) fusion(bf16[2,64,16,1024]{3,2,1,0:T(8,128)(2,1)} %bitcast.158), kind=kLoop, calls=%fused_computation.105 | loop fusion | bytes 8388608 | tf_op jit(solution)/shard_map/transpose | solution.py:324
  278.7 8.8 %add_convert_fusion.3 = bf16[1024,512]{1,0:T(8,128)(2,1)} fusion(bf16[2048,512]{1,0:T(8,128)(2,1)} %bitcast.166, bf16[512,2048]{1,0:T(8,128)(2,1)} %reshape.336, bf16[2,1,1024,512]{3,2,1,0:T(8,128)(2,1)} %param.15), kind=kOutput, calls=%fused_computation.128 | convolution fusion | flops 4315414528 | bytes 7340032 | tf_op jit(solution)/shard_map/bsf,fd->bsd/dot_general | solution.py:50
  289.0 4.0 %slice_bitcast_fusion.3 = (bf16[64,8,2,2,512]{4,1,3,0,2:T(8,128)(2,1)S(1)}, bf16[64,2,16,512]{3,2,0,1:T(8,128)(2,1)}) fusion(bf16[2,64,16,1024]{3,2,1,0:T(8,128)(2,1)} %bitcast.157), kind=kLoop, calls=%fused_computation.101 | loop fusion | bytes 8388608 | tf_op jit(solution)/shard_map/transpose | solution.py:324
  301.4 8.7 %add_convert_fusion.1 = bf16[1024,512]{1,0:T(8,128)(2,1)} fusion(bf16[2048,512]{1,0:T(8,128)(2,1)} %bitcast.167, bf16[512,2048]{1,0:T(8,128)(2,1)} %reshape.342, bf16[2,1,1024,512]{3,2,1,0:T(8,128)(2,1)} %param.15), kind=kOutput, calls=%fused_computation.126 | convolution fusion | flops 4315414528 | bytes 7340032 | tf_op jit(solution)/shard_map/bsf,fd->bsd/dot_general | solution.py:50
  310.1 6.9 %fusion.147 = bf16[1,1,1024,512]{3,2,1,0:T(8,128)(2,1)S(1)} fusion(bf16[2048,512]{1,0:T(8,128)(2,1)} %bitcast.164, bf16[1024,512]{1,0:T(8,128)(2,1)} %add_convert_fusion.1, bf16[512,2048]{1,0:T(8,128)(2,1)S(1)} %copy-done.1), kind=kOutput, calls=%fused_computation.146 | convolution fusion | flops 4315414528 | bytes 6291456 | tf_op jit(solution)/shard_map/bsf,fd->bsd/dot_general | solution.py:50
  317.1 4.0 %slice_bitcast_fusion.5 = (bf16[64,8,2,2,512]{4,1,3,0,2:T(8,128)(2,1)S(1)}, bf16[64,2,16,512]{3,2,0,1:T(8,128)(2,1)}) fusion(bf16[2,64,16,1024]{3,2,1,0:T(8,128)(2,1)} %bitcast.156), kind=kLoop, calls=%fused_computation.103 | loop fusion | bytes 8388608 | tf_op jit(solution)/shard_map/transpose | solution.py:324
  328.2 8.0 %fusion.144 = bf16[1,1,1024,512]{3,2,1,0:T(8,128)(2,1)} fusion(bf16[2048,512]{1,0:T(8,128)(2,1)S(1)} %bitcast.165, bf16[1024,512]{1,0:T(8,128)(2,1)} %add_convert_fusion.3, bf16[512,2048]{1,0:T(8,128)(2,1)} %reshape.339), kind=kOutput, calls=%fused_computation.145 | convolution fusion | flops 4315414528 | bytes 6291456 | tf_op jit(solution)/shard_map/bsf,fd->bsd/dot_general | solution.py:50
  (41 shorter events, 44.0 us)
Async XLA Ops:
  0.6 4.4 %copy-start.5 = (bf16[2,2,512,2048]{3,2,1,0:T(8,128)(2,1)S(1)}, bf16[2,2,512,2048]{3,2,1,0:T(8,128)(2,1)}, u32[]{:S(2)}) copy-start(bf16[2,2,512,2048]{3,2,1,0:T(8,128)(2,1)} %param.16) | copy-start | bytes 25165828
  5.1 24.9 %copy-start.8 = (f32[1024,2048]{1,0:T(8,128)}, f32[1024,2048]{1,0:T(8,128)S(1)}, u32[]{:S(2)}) copy-start(f32[1024,2048]{1,0:T(8,128)S(1)} %fusion.106) | copy-start | bytes 25165828
  5.1 4.5 %copy-start.7 = (bf16[2,1,1024,512]{3,2,1,0:T(8,128)(2,1)S(1)}, bf16[2,1,1024,512]{3,2,1,0:T(8,128)(2,1)}, u32[]{:S(2)}) copy-start(bf16[2,1,1024,512]{3,2,1,0:T(8,128)(2,1)} %param.14) | copy-start | bytes 6291460
  46.4 4.4 %copy-start.6 = (bf16[2,2,1,1024,512]{4,3,2,1,0:T(8,128)(2,1)S(1)}, bf16[2,2,1,1024,512]{4,3,2,1,0:T(8,128)(2,1)}, u32[]{:S(2)}) copy-start(bf16[2,2,1,1024,512]{4,3,2,1,0:T(8,128)(2,1)} %param.13) | copy-start | bytes 12582916
  50.8 25.9 %copy-start.9 = (f32[1024,2048]{1,0:T(8,128)}, f32[1024,2048]{1,0:T(8,128)S(1)}, u32[]{:S(2)}) copy-start(f32[1024,2048]{1,0:T(8,128)S(1)} %fusion.94) | copy-start | bytes 25165828
  278.7 8.8 %copy-start = (bf16[64,2,16,512]{3,2,0,1:T(8,128)(2,1)S(1)}, bf16[64,2,16,512]{3,2,0,1:T(8,128)(2,1)}, u32[]{:S(2)}) copy-start(bf16[64,2,16,512]{3,2,0,1:T(8,128)(2,1)} %get-tuple-element.30) | copy-start | bytes 6291460
  301.4 8.7 %copy-start.1 = (bf16[512,2048]{1,0:T(8,128)(2,1)S(1)}, bf16[512,2048]{1,0:T(8,128)(2,1)}, u32[]{:S(2)}) copy-start(bf16[512,2048]{1,0:T(8,128)(2,1)} %reshape.345) | copy-start | bytes 6291460
  328.1 15.5 %copy-start.4 = (f32[2,2,16,512]{3,2,1,0:T(8,128)S(1)}, f32[2,2,16,512]{3,2,1,0:T(8,128)}, u32[]{:S(2)}) copy-start(f32[2,2,16,512]{3,2,1,0:T(8,128)} %get-tuple-element.43) | copy-start | bytes 393220
  328.2 16.1 %copy-start.3 = (f32[2,2,4,2048]{3,2,1,0:T(4,128)S(1)}, f32[2,2,4,2048]{3,2,1,0:T(4,128)}, u32[]{:S(2)}) copy-start(f32[2,2,4,2048]{3,2,1,0:T(4,128)} %get-tuple-element.44) | copy-start | bytes 393220
  328.2 16.7 %copy-start.2 = (f32[2,2,16,512]{3,2,1,0:T(8,128)S(1)}, f32[2,2,16,512]{3,2,1,0:T(8,128)}, u32[]{:S(2)}) copy-start(f32[2,2,16,512]{3,2,1,0:T(8,128)} %get-tuple-element.45) | copy-start | bytes 393220

commit v2 on v1

v2 whole, which is shorter than its diff:
```python
import jax
import jax.numpy as jnp
from jax import lax
from jax.experimental import pallas as pl
from jax.experimental.pallas import tpu as pltpu
from jax.sharding import PartitionSpec as P

LEARN_RATE = 0.005
BETA_ONE = 0.9
BETA_TWO = 0.95
ADAM_EPS = 1e-8
WEIGHT_DECAY = 0.1
MICROBATCHES = 2
ADAM_STEP = 2
MESH = pl.DeviceIdType.MESH

ORDERS = ((2, 1, 0), (1, 0, 2), (0, 2, 1))
RS_LANES = ((0, 768), (768, 640), (1408, 640))
AG_LANES = ((0, 384), (384, 384), (768, 256))
TASKS = ((0, 1), (0, 0), (1, 1), (1, 0))
TILES = 8
RING = 4
SUB = 8
ROWS = 16
DIM = 512
HALF = 1024
FF = 2048
WIDTH = 256
OFFSETS = (0, 2, 6, 13, 17, 20, 21, 22, 24, 27, 32, 35, 39)
FORWARD = ((1, 0, 0), (0, 0, 1), (3, 1, 0), (2, 1, 1))
GELU_A = 0.7978845608028654
GELU_B = GELU_A * 0.044715


def adam_update(acc_part, grad_new, master, moment_one, moment_two):
    grad_mean = (acc_part + grad_new) / MICROBATCHES
    moment_one = BETA_ONE * moment_one + (1.0 - BETA_ONE) * grad_mean
    moment_two = BETA_TWO * moment_two + (1.0 - BETA_TWO) * grad_mean * grad_mean
    corr_one = 1.0 - BETA_ONE ** ADAM_STEP
    corr_two = 1.0 - BETA_TWO ** ADAM_STEP
    step_dir = (moment_one / corr_one) / (jnp.sqrt(moment_two / corr_two) + ADAM_EPS)
    master = master - LEARN_RATE * (step_dir + WEIGHT_DECAY * master)
    return master, moment_one, moment_two


def mm(a, b, a_dim, b_dim):
    return lax.dot_general(a, b, (((a_dim,), (b_dim,)), ((), ())), preferred_element_type=jnp.float32)


def half_dim(axis):
    return 1 if axis == 0 else 0


def region(fixed, lanes):
    return tuple(fixed.get(dim, slice(None)) for dim in range(3)) + (slice(None), pl.ds(lanes[0], lanes[1]))


def step_kernel(*refs):
    x_saved, grad_out, x_next, w_up, w_down = refs[0:5]
    acc_up, acc_down, master_up, master_down, m1_up, m1_down, m2_up, m2_down = refs[5:13]
    out_states = refs[13:19]
    y_out = refs[19]
    (wu, wd, xbuf, cot, total, plane, rs1, rs2, rs3, rs4, grad_x, part_x, block8, gath, w_sem, x_sem, send_sem, recv_sem, free_sem) = refs[20:]

    me = lax.axis_index('fsdp')
    core = lax.rem(me, 2)
    chip = lax.div(me, 2)
    pos = (lax.div(chip, ROWS), lax.rem(lax.div(chip, RING), RING), lax.rem(chip, RING))
    stride = (32, SUB, 2)
    partner = me + 1 - 2 * core
    near = [[lax.rem(pos[axis] + step, RING) for step in range(RING)] for axis in range(3)]
    peers = [[me + (near[axis][step] - pos[axis]) * stride[axis] for step in range(RING)] for axis in range(3)]

    def tile_of(i):
        return lax.rem(i + RING * (1 - core), TILES)

    def weight_copies(t, i):
        s, l = TASKS[t]
        cols = pl.ds(pl.multiple_of(tile_of(i) * WIDTH, WIDTH), WIDTH)
        return (pltpu.make_async_copy(w_up.at[s, l, :, cols], wu.at[i], w_sem.at[0, i]),
                pltpu.make_async_copy(w_down.at[s, l, cols, :], wd.at[i], w_sem.at[1, i]))

    def x_copy(t):
        s, l = TASKS[t]
        return pltpu.make_async_copy(x_saved.at[s, l, 0], xbuf.at[t % 2], x_sem.at[t % 2])

    def next_copy(s):
        return pltpu.make_async_copy(x_next.at[s, 0], xbuf.at[s], x_sem.at[s])

    def cot_copy(s):
        return pltpu.make_async_copy(grad_out.at[s, 0], cot.at[s], x_sem.at[2 + s])

    def y_copy(s):
        return pltpu.make_async_copy(xbuf.at[s], y_out.at[s, 0], x_sem.at[RING + s])

    x_copy(0).start()
    cot_copy(0).start()

    def first_weights(i, carry):
        for copy in weight_copies(0, i):
            copy.start()
        return carry

    lax.fori_loop(0, TILES, first_weights, 0)
    x_copy(1).start()
    cot_copy(1).start()

    barrier = pltpu.get_barrier_semaphore()
    pl.semaphore_signal(barrier, inc=1, device_id=(partner,), device_id_type=MESH)
    for axis in range(3):
        for step in (1, 2, 3):
            pl.semaphore_signal(barrier, inc=1, device_id=(peers[axis][step],), device_id_type=MESH)
    pl.semaphore_wait(barrier, 10)

    class Task:
        def __init__(self, task_id):
            self.t = task_id
            self.par = task_id % 2
            self.slot = 0
            self.live = []
            self.stage, self.layer = TASKS[task_id]

        def send(self, src, dst, device):
            slot = self.slot
            self.slot += 1

            def make():
                return pltpu.make_async_remote_copy(src_ref=src(), dst_ref=dst(), send_sem=send_sem.at[self.t, slot], recv_sem=recv_sem.at[self.t, slot], device_id=(device,), device_id_type=MESH)

            make().start()
            self.live.append(make)

        def drain(self):
            for make in self.live:
                make().wait()
            self.live = []

        def plane_at(self, fixed, g):
            return lambda: plane.at[(self.t,) + region(fixed, RS_LANES[g])]

        def gath_at(self, fixed, g):
            return lambda: gath.at[(self.t, core) + region(fixed, AG_LANES[g])]

        def run(self, phase):
            getattr(self, 'phase_%s' % phase)()

        def phase_up(self):
            self.send(lambda: gath.at[self.t, 1, 0:2], lambda: gath.at[self.t, 0, 0:2], partner)

        def phase_0(self):
            self.send(lambda: gath.at[self.t, 1, 2:RING], lambda: gath.at[self.t, 0, 2:RING], partner)

        def phase_1(self):
            t, par = self.t, self.par
            self.drain()

            def body(i, carry):
                z_pos, y_pos = lax.div(i, RING), lax.rem(i, RING)
                z_blk, y_blk, x_blk = lax.div(i, SUB), lax.div(lax.rem(i, SUB), 2), 2 * lax.rem(i, 2)
                up_part = gath[t, 0, z_blk, y_blk, pl.ds(x_blk, 2)].astype(jnp.float32)
                plane[t, z_pos, y_pos, :, :, 0:HALF] = plane[t, z_pos, y_pos, :, :, 0:HALF] + up_part.reshape(RING, SUB, HALF)
                down_part = gath[t, 0, z_blk + 2, y_blk, pl.ds(x_blk, 2)].astype(jnp.float32)
                for k in range(2):
                    for m in range(2):
                        for h in range(2):
                            lanes = slice(HALF + DIM * h, HALF + DIM * (h + 1))
                            plane[t, z_pos, y_pos, 2 * k + m, :, lanes] = plane[t, z_pos, y_pos, 2 * k + m, :, lanes] + down_part[k, SUB * h:SUB * h + SUB, DIM * m:DIM * m + DIM]
                return carry

            lax.fori_loop(0, ROWS, body, 0)
            for g, order in enumerate(ORDERS):
                axis, half = order[0], half_dim(order[0])
                lanes = pl.ds(*RS_LANES[g])
                for way, step in ((0, 1), (1, 3)):
                    self.send(self.plane_at({axis: near[axis][2], half: pl.ds(2 * way, 2)}, g), lambda way=way, lanes=lanes: rs1.at[par, way, :, :, :, lanes], peers[axis][step])

        def phase_2(self):
            t, par = self.t, self.par
            self.drain()
            for g, order in enumerate(ORDERS):
                axis, half = order[0], half_dim(order[0])
                lanes = pl.ds(*RS_LANES[g])
                for way, step in ((0, 1), (1, 3)):
                    where = (t,) + region({axis: near[axis][step], half: pl.ds(2 * way, 2)}, RS_LANES[g])
                    plane[where] = plane[where] + rs1[par, way, :, :, :, lanes]
            for g, order in enumerate(ORDERS):
                axis = order[0]
                lanes = pl.ds(*RS_LANES[g])
                for way, step in ((0, 1), (1, 3)):
                    if t >= 2:
                        pl.semaphore_wait(free_sem.at[0, par, g, way], 1)
                    self.send(self.plane_at({axis: near[axis][step]}, g), lambda way=way, lanes=lanes: rs2.at[par, way, :, :, :, lanes], peers[axis][step])

        def phase_3(self):
            t, par = self.t, self.par
            self.drain()
            for g, order in enumerate(ORDERS):
                lanes = pl.ds(*RS_LANES[g])
                where = (t,) + region({order[0]: pos[order[0]]}, RS_LANES[g])
                plane[where] = plane[where] + (rs2[par, 0, :, :, :, lanes] + rs2[par, 1, :, :, :, lanes])
                if t < 2:
                    for way, step in ((0, 3), (1, 1)):
                        pl.semaphore_signal(free_sem.at[0, par, g, way], inc=1, device_id=(peers[order[0]][step],), device_id_type=MESH)
            for g, order in enumerate(ORDERS):
                lanes = pl.ds(*RS_LANES[g])
                axis = order[1]
                for step in (1, 2, 3):
                    if t >= 2:
                        pl.semaphore_wait(free_sem.at[1, par, g, step - 1], 1)
                    self.send(self.plane_at({order[0]: pos[order[0]], axis: near[axis][step]}, g), lambda step=step, lanes=lanes: rs3.at[par, step - 1, :, :, lanes], peers[axis][step])

        def phase_4(self):
            t, par = self.t, self.par
            self.drain()
            for g, order in enumerate(ORDERS):
                lanes = pl.ds(*RS_LANES[g])
                where = (t,) + region({order[0]: pos[order[0]], order[1]: pos[order[1]]}, RS_LANES[g])
                plane[where] = plane[where] + (rs3[par, 0, :, :, lanes] + rs3[par, 1, :, :, lanes] + rs3[par, 2, :, :, lanes])
                if t < 2:
                    for step in (1, 2, 3):
                        pl.semaphore_signal(free_sem.at[1, par, g, step - 1], inc=1, device_id=(peers[order[1]][RING - step],), device_id_type=MESH)
            for g, order in enumerate(ORDERS):
                lanes = pl.ds(*RS_LANES[g])
                axis = order[2]
                fixed = {order[0]: pos[order[0]], order[1]: pos[order[1]]}
                for step in (1, 2, 3):
                    self.send(self.plane_at({**fixed, axis: near[axis][step]}, g), lambda step=step, lanes=lanes: rs4.at[t, step - 1, :, lanes], peers[axis][step])

        def phase_5(self):
            t = self.t
            self.drain()
            block = plane[t, pos[0], pos[1], pos[2]] + (rs4[t, 0] + rs4[t, 1] + rs4[t, 2])
            block8[t] = block
            grad_x[t, core] = block[:, 0:HALF]
            self.send(lambda: grad_x.at[t, core], lambda: grad_x.at[t, core], partner)

        def phase_6(self):
            t, s, l = self.t, self.stage, self.layer
            self.drain()
            grad_down = jnp.concatenate([block8[t, :, HALF:HALF + DIM], block8[t, :, HALF + DIM:FF]], axis=0)
            new_down = adam_update(acc_down[s, l], grad_down, master_down[s, l], m1_down[s, l], m2_down[s, l])
            low = jnp.concatenate([grad_x[t, 0, 0:RING, :], grad_x[t, 1, 0:RING, :]], axis=1)
            high = jnp.concatenate([grad_x[t, 0, RING:SUB, :], grad_x[t, 1, RING:SUB, :]], axis=1)
            grad_up = jnp.where(core == 0, low, high)
            new_up = adam_update(acc_up[s, l], grad_up, master_up[s, l], m1_up[s, l], m2_up[s, l])
            for i in range(3):
                out_states[2 * i][s, l] = new_up[i]
                out_states[2 * i + 1][s, l] = new_down[i]
            left, right = new_up[0][:, 0:HALF], new_up[0][:, HALF:FF]
            part_x[t, core] = jnp.where(core == 0, left, right)
            part_x[t, 2] = jnp.where(core == 0, right, left)
            self.send(lambda: part_x.at[t, 2], lambda: part_x.at[t, core], partner)
            gath[t, core, pos[0], pos[1], pos[2], :, DIM:HALF] = new_down[0].astype(jnp.bfloat16)

        def phase_7(self):
            t = self.t
            self.drain()
            block8[t, 0:RING, 0:HALF] = part_x[t, 0]
            block8[t, RING:SUB, 0:HALF] = part_x[t, 1]
            rows = jnp.concatenate([block8[t, :, 0:DIM], block8[t, :, DIM:HALF]], axis=0)
            gath[t, core, pos[0], pos[1], pos[2], :, 0:DIM] = rows.astype(jnp.bfloat16)
            for g, order in enumerate(ORDERS):
                where = self.gath_at({0: pos[0], 1: pos[1], 2: pos[2]}, g)
                for step in (1, 2, 3):
                    self.send(where, where, peers[order[2]][step])

        def phase_8(self):
            self.drain()
            for g, order in enumerate(ORDERS):
                where = self.gath_at({order[0]: pos[order[0]], order[1]: pos[order[1]]}, g)
                for step in (1, 2, 3):
                    self.send(where, where, peers[order[1]][step])

        def phase_9(self):
            self.drain()
            for g, order in enumerate(ORDERS):
                where = self.gath_at({order[0]: pos[order[0]]}, g)
                for step in (1, 3):
                    self.send(where, where, peers[order[0]][step])

        def phase_10(self):
            self.drain()
            for g, order in enumerate(ORDERS):
                axis, half = order[0], half_dim(order[0])
                for way, step in ((0, 1), (1, 3)):
                    where = self.gath_at({axis: near[axis][RING - step], half: pl.ds(2 * way, 2)}, g)
                    self.send(where, where, peers[axis][step])

        def phase_11(self):
            self.drain()
            self.send(lambda: gath.at[self.t, core], lambda: gath.at[self.t, core], partner)

        def phase_12(self):
            self.drain()

    tasks = [Task(t) for t in range(RING)]
    agenda = sorted((TILES * (t + 1) - 1 + offset, t, phase) for t in range(RING) for phase, offset in enumerate(OFFSETS))
    finished = set()

    def advance(now):
        while agenda and agenda[0][0] <= now:
            _, t, phase = agenda.pop(0)
            tasks[t].run(phase)
            finished.add((t, phase))

    def backward(t):
        s, l = TASKS[t]
        slot = t % 2
        x_copy(t).wait()
        if l == 1:
            cot_copy(s).wait()
            total[...] = jnp.zeros_like(total)

        def body(i, carry):
            j = tile_of(i)
            for copy in weight_copies(t, i):
                copy.wait()
            x, dy, w1, w2 = xbuf[slot], cot[s], wu[i], wd[i]
            h = mm(x, w1, 1, 0)
            grad_act = mm(dy, w2, 1, 1)
            square = h * h
            tanh = jnp.tanh(h * (GELU_A + GELU_B * square))
            gate = 0.5 * tanh + 0.5
            act = (h * gate).astype(jnp.bfloat16)
            slope = gate + (0.5 * h) * (1.0 - tanh * tanh) * (GELU_A + 3.0 * GELU_B * square)
            grad_h = (grad_act * slope).astype(jnp.bfloat16)
            down = mm(act, dy, 0, 0).reshape(SUB, 2, ROWS, DIM)
            own = jnp.where(core == 0, down[:, 0], down[:, 1])
            other = jnp.where(core == 0, down[:, 1], down[:, 0]).astype(jnp.bfloat16)
            rows = pl.ds(2 * lax.rem(j, 2), 2)
            plane[t, lax.div(j, 2), rows, :, :, HALF:HALF + DIM] = own[:, 0:SUB].reshape(2, RING, SUB, DIM)
            plane[t, lax.div(j, 2), rows, :, :, HALF + DIM:FF] = own[:, SUB:ROWS].reshape(2, RING, SUB, DIM)
            for k in range(RING):
                gath[t, 1, 2 + lax.div(j, RING), lax.rem(j, RING), k, :, 0:DIM] = other[2 * k]
                gath[t, 1, 2 + lax.div(j, RING), lax.rem(j, RING), k, :, DIM:HALF] = other[2 * k + 1]
            up = mm(x, grad_h, 0, 0)
            cols = pl.ds(pl.multiple_of(lax.rem(j, RING) * WIDTH, WIDTH), WIDTH)

            @pl.when(i < RING)
            def _():
                gath[t, 1, 0:2, :, :, :, cols] = up.astype(jnp.bfloat16).reshape(2, RING, RING, ROWS, WIDTH)

            @pl.when(i >= RING)
            def _():
                plane[t, :, :, :, :, cols] = up.reshape(RING, RING, RING, SUB, WIDTH)

            if l == 1:
                total[...] = total[...] + mm(grad_h, w1, 1, 1)
            if t < 3:
                for copy in weight_copies(t + 1, i):
                    copy.start()

            for k in range(TILES):
                if k == 3 or agenda and agenda[0][0] <= TILES * t + k:
                    @pl.when(i == k)
                    def _():
                        if k == 3:
                            tasks[t].run('up')
                        advance(TILES * t + k)
            return carry

        lax.fori_loop(0, TILES, body, 0)
        if l == 1:
            cot[s] = (cot[s].astype(jnp.float32) + total[...]).astype(jnp.bfloat16)
        if t < 2:
            x_copy(t + 2).start()
        else:
            next_copy(t - 2).start()

    def forward(t, s, l, now):
        if l == 0:
            next_copy(s).wait()
        total[...] = jnp.zeros_like(total)

        def body(i, carry):
            half, q, lane = lax.div(i, RING), lax.div(lax.rem(i, RING), 2), lax.rem(i, 2)
            lanes = pl.ds(pl.multiple_of(lane * WIDTH, WIDTH), WIDTH)
            raw = gath[t, half, :, :, :, :, lanes].astype(jnp.float32).reshape(64, ROWS, WIDTH)
            w1 = jnp.where(q == 0, raw[:, 0:SUB], raw[:, SUB:ROWS]).reshape(DIM, WIDTH).astype(jnp.bfloat16)
            rows = pl.ds(2 * lax.rem(i, 2), 2)
            even = gath[t, 0, lax.div(i, 2), rows, :, :, DIM:HALF].reshape(SUB, 1, ROWS, DIM)
            odd = gath[t, 1, lax.div(i, 2), rows, :, :, DIM:HALF].reshape(SUB, 1, ROWS, DIM)
            w2 = jnp.concatenate([even, odd], axis=1).reshape(WIDTH, DIM)
            h = mm(xbuf[s], w1, 1, 0)
            tanh = jnp.tanh(h * (GELU_A + GELU_B * (h * h)))
            act = (h * (0.5 * tanh + 0.5)).astype(jnp.bfloat16)
            total[...] = total[...] + mm(act, w2, 1, 0)
            for k in range(1, TILES, 2):
                if agenda and agenda[0][0] <= now + k // 2:
                    @pl.when(i == k)
                    def _():
                        advance(now + k // 2)
            return carry

        lax.fori_loop(0, TILES, body, 0)
        xbuf[s] = (xbuf[s].astype(jnp.float32) + total[...]).astype(jnp.bfloat16)
        if l == 1:
            y_copy(s).start()
        return now + TILES // 2

    for t in range(RING):
        backward(t)
    now = RING * TILES - 1
    for t, s, l in FORWARD:
        while (t, 12) not in finished:
            now = max(now, agenda[0][0])
            advance(agenda[0][0])
        now = forward(t, s, l, now)
    for s in range(2):
        y_copy(s).wait()


def fused_step(*args):
    vmem = pl.BlockSpec(memory_space=pltpu.VMEM)
    hbm = pl.BlockSpec(memory_space=pl.ANY)
    up_state = jax.ShapeDtypeStruct(args[5].shape, jnp.float32)
    down_state = jax.ShapeDtypeStruct(args[6].shape, jnp.float32)
    scratch = [
        pltpu.VMEM((TILES, DIM, WIDTH), jnp.bfloat16),
        pltpu.VMEM((TILES, WIDTH, DIM), jnp.bfloat16),
        pltpu.VMEM((2, HALF, DIM), jnp.bfloat16),
        pltpu.VMEM((2, HALF, DIM), jnp.bfloat16),
        pltpu.VMEM((HALF, DIM), jnp.float32),
        pltpu.VMEM((RING,) * RING + (SUB, FF), jnp.float32),
        pltpu.VMEM((2, 2, 2, RING, SUB, FF), jnp.float32),
        pltpu.VMEM((2, 2, RING, RING, SUB, FF), jnp.float32),
        pltpu.VMEM((2, 3, RING, SUB, FF), jnp.float32),
        pltpu.VMEM((RING, 3, SUB, FF), jnp.float32),
        pltpu.VMEM((RING, 2, SUB, HALF), jnp.float32),
        pltpu.VMEM((RING, 3, RING, HALF), jnp.float32),
        pltpu.VMEM((RING, SUB, FF), jnp.float32),
        pltpu.VMEM((RING, 2, RING, RING, RING, ROWS, HALF), jnp.bfloat16),
        pltpu.SemaphoreType.DMA((2, TILES)),
        pltpu.SemaphoreType.DMA((6,)),
        pltpu.SemaphoreType.DMA((RING, 66)),
        pltpu.SemaphoreType.DMA((RING, 66)),
        pltpu.SemaphoreType.REGULAR((2, 2, 3, 3)),
    ]
    return pl.pallas_call(
        step_kernel,
        out_shape=(up_state, down_state) * 3 + (jax.ShapeDtypeStruct(args[2].shape, jnp.bfloat16),),
        in_specs=[hbm] * 5 + [vmem] * SUB,
        out_specs=(vmem,) * 6 + (hbm,),
        scratch_shapes=scratch,
        compiler_params=pltpu.CompilerParams(collective_id=0, has_side_effects=True, vmem_limit_bytes=67043328),
        name='step',
    )(*args)


def solution(mesh):
    tok_spec = P(None, 'fsdp')
    layer_spec = P(None, None, 'fsdp')
    rep_spec = P()

    def device_step(*args):
        return tuple(fused_step(*args))

    return jax.shard_map(device_step, mesh=mesh, in_specs=(layer_spec, tok_spec, tok_spec, rep_spec, rep_spec) + (layer_spec,) * SUB, out_specs=(layer_spec,) * 6 + (tok_spec,), check_vma=False)
```

time: 349 us -> 206 us (0.59)
  matrix products: 125 us -> 0 us
  local copies, waits for them, and re-layouts: 62.3 us -> 12.4 us
  Pallas kernels: 155 us -> 192 us
    dot_general x20 -> x0, matrix products: 125 us -> none  [the longest x4 33.3 us: backward_layer(): jnp.einsum('bsd,bsf->df', x_in, grad_hidden, preferred_element_type=jnp.f...]
    pallas_call x1, Pallas kernels: 155 us -> 192 us  [fused_step(): pl.pallas_call(step_kernel, out_shape=(up_state, down_state) * 3 + (jax.S...]
    transpose x12 -> x0, local copies, waits for them, and re-layouts: 32.2 us -> none  [the longest x8 22.4 us: device_step(): part[:, :, :, :512].reshape(2, 64, 2, 8, 512).transpose(1, 3, 0, 2, 4)]
    reshape x4 -> x0, local copies, waits for them, and re-layouts: 11.9 us -> none  [device_step(): part[:, :, :, :512].reshape(2, 64, 2, 8, 512).transpose(1, 3, 0, 2, 4)]
    slice x1 -> x0, local copies, waits for them, and re-layouts: 11.5 us -> none  [device_step(): part = gath[TASKS.index((stage_id, layer_id))]]
    unnamed x26 -> x7, local copies, waits for them, and re-layouts: 6.71 us -> 12.4 us
where the time goes in v2:
time: 206 us; the launch traced here: 205 us
  Pallas kernels  192 us (93%)
  local copies, waits for them, and re-layouts  12.4 us (6%)
    pallas_call x1, Pallas kernels, fused_step(): pl.pallas_call(step_kernel, out_shape=(up_state, down_state) * 3 + (jax.S...  192 us
    unnamed x7, local copies, waits for them, and re-layouts  12.4 us

profile of v2, /device:TPU:1, one launch (start us, length us, event | category | flops | bytes accessed | tf_op | source)
XLA Modules:
  0.0 205.4 jit_solution(12633177724987548186)
XLA Ops:
  0.6 192.3 %step.1 = (f32[2,2,4,2048]{3,2,1,0:T(4,128)}, f32[2,2,16,512]{3,2,1,0:T(8,128)}, f32[2,2,4,2048]{3,2,1,0:T(4,128)}, f32[2,2,16,512]{3,2,1,0:T(8,128)}, f32[2,2,4...) custom-call(bf16[2,2,1,1024,512]{4,3,2,1,0:T(8,128)(2,1)} %refs_0_.1, ...), custom_call_target="tpu_custom_call" | custom-call | tf_op jit(solution)/shard_map/step/pallas_call | solution.py:439
  193.0 1.6 copy.27
  194.5 1.6 copy.28
  196.1 1.6 copy.29
  197.7 1.6 copy.30
  199.2 1.6 copy.31
  200.8 1.6 copy.32
  202.4 3.0 %copy.33 = bf16[2,1,1024,512]{3,2,1,0:T(8,128)(2,1)} copy(bf16[2,1,1024,512]{3,2,1,0:T(8,128)(2,1)} %get-tuple-element.20) | data formatting | bytes 4194304

commit v3 on v2

--- a/solution.py
+++ b/solution.py
@@ -19,6 +19,8 @@
 AG_LANES = ((0, 384), (384, 384), (768, 256))
 TASKS = ((0, 1), (0, 0), (1, 1), (1, 0))
 TILES = 8
+CHUNK = 512
+SPAN = 256
 RING = 4
 SUB = 8
 ROWS = 16
@@ -60,7 +62,7 @@
     acc_up, acc_down, master_up, master_down, m1_up, m1_down, m2_up, m2_down = refs[5:13]
     out_states = refs[13:19]
     y_out = refs[19]
-    (wu, wd, xbuf, cot, total, plane, rs1, rs2, rs3, rs4, grad_x, part_x, block8, gath, w_sem, x_sem, send_sem, recv_sem, free_sem) = refs[20:]
+    (wu, wd, xbuf, cot, total, act_buf, grad_buf, plane, rs1, rs2, rs3, rs4, grad_x, part_x, block8, gath, w_sem, x_sem, send_sem, recv_sem, free_sem) = refs[20:]
 
     me = lax.axis_index('fsdp')
     core = lax.rem(me, 2)
@@ -311,55 +313,85 @@
             cot_copy(s).wait()
             total[...] = jnp.zeros_like(total)
 
-        def body(i, carry):
-            j = tile_of(i)
+        def fetch(i):
             for copy in weight_copies(t, i):
                 copy.wait()
-            x, dy, w1, w2 = xbuf[slot], cot[s], wu[i], wd[i]
-            h = mm(x, w1, 1, 0)
-            grad_act = mm(dy, w2, 1, 1)
+
+        def front(i, m):
+            rows = pl.ds(m * CHUNK, CHUNK)
+            h = mm(xbuf[slot, rows, :], wu[i], 1, 0)
+            grad_act = mm(cot[s, rows, :], wd[i], 1, 1)
             square = h * h
             tanh = jnp.tanh(h * (GELU_A + GELU_B * square))
             gate = 0.5 * tanh + 0.5
-            act = (h * gate).astype(jnp.bfloat16)
+            act_buf[lax.rem(i, 2), rows, :] = (h * gate).astype(jnp.bfloat16)
             slope = gate + (0.5 * h) * (1.0 - tanh * tanh) * (GELU_A + 3.0 * GELU_B * square)
-            grad_h = (grad_act * slope).astype(jnp.bfloat16)
-            down = mm(act, dy, 0, 0).reshape(SUB, 2, ROWS, DIM)
+            grad_buf[lax.rem(i, 2), rows, :] = (grad_act * slope).astype(jnp.bfloat16)
+
+        def back_down(i, n):
+            j = tile_of(i)
+            lanes = pl.ds(n * WIDTH, WIDTH)
+            down = mm(act_buf[lax.rem(i, 2)], cot[s, :, lanes], 0, 0).reshape(SUB, 2, ROWS, WIDTH)
             own = jnp.where(core == 0, down[:, 0], down[:, 1])
             other = jnp.where(core == 0, down[:, 1], down[:, 0]).astype(jnp.bfloat16)
             rows = pl.ds(2 * lax.rem(j, 2), 2)
-            plane[t, lax.div(j, 2), rows, :, :, HALF:HALF + DIM] = own[:, 0:SUB].reshape(2, RING, SUB, DIM)
-            plane[t, lax.div(j, 2), rows, :, :, HALF + DIM:FF] = own[:, SUB:ROWS].reshape(2, RING, SUB, DIM)
-            for k in range(RING):
-                gath[t, 1, 2 + lax.div(j, RING), lax.rem(j, RING), k, :, 0:DIM] = other[2 * k]
-                gath[t, 1, 2 + lax.div(j, RING), lax.rem(j, RING), k, :, DIM:HALF] = other[2 * k + 1]
-            up = mm(x, grad_h, 0, 0)
-            cols = pl.ds(pl.multiple_of(lax.rem(j, RING) * WIDTH, WIDTH), WIDTH)
-
-            @pl.when(i < RING)
-            def _():
-                gath[t, 1, 0:2, :, :, :, cols] = up.astype(jnp.bfloat16).reshape(2, RING, RING, ROWS, WIDTH)
-
-            @pl.when(i >= RING)
-            def _():
-                plane[t, :, :, :, :, cols] = up.reshape(RING, RING, RING, SUB, WIDTH)
-
-            if l == 1:
-                total[...] = total[...] + mm(grad_h, w1, 1, 1)
+            for h in range(2):
+                plane[t, lax.div(j, 2), rows, :, :, pl.ds(HALF + h * DIM + n * WIDTH, WIDTH)] = own[:, h * SUB:(h + 1) * SUB].reshape(2, RING, SUB, WIDTH)
+            for k in range(SUB):
+                gath[t, 1, 2 + lax.div(j, RING), lax.rem(j, RING), k // 2, :, pl.ds(k % 2 * DIM + n * WIDTH, WIDTH)] = other[k]
+
+        def back_up(i, n, mine):
+            up = mm(xbuf[slot, :, pl.ds(n * WIDTH, WIDTH)], grad_buf[lax.rem(i, 2)], 0, 0)
+            cols = pl.ds(pl.multiple_of(lax.rem(tile_of(i), RING) * WIDTH, WIDTH), WIDTH)
+            if mine:
+                plane[t, pl.ds(2 * n, 2), :, :, :, cols] = up.reshape(2, RING, RING, SUB, WIDTH)
+            else:
+                gath[t, 1, n, :, :, :, cols] = up.astype(jnp.bfloat16).reshape(RING, RING, ROWS, WIDTH)
+
+        def back_dx(i, m):
+            rows = pl.ds(m * CHUNK, CHUNK)
+            total[rows, :] = total[rows, :] + mm(grad_buf[lax.rem(i, 2), rows, :], wu[i], 1, 1)
+
+        def events(k):
+            if k == 3:
+                tasks[t].run('up')
+            advance(TILES * t + k)
+
+        def tile(i, mine, ahead):
+            if ahead:
+                fetch(i + 1)
+            for m in range(HALF // CHUNK):
+                if ahead:
+                    front(i + 1, m)
+                for n in range(2):
+                    if m == n * (HALF // CHUNK // 2):
+                        back_down(i, n)
+                        back_up(i, n, mine)
+                if l == 1:
+                    back_dx(i, m)
             if t < 3:
                 for copy in weight_copies(t + 1, i):
                     copy.start()
 
-            for k in range(TILES):
-                if k == 3 or agenda and agenda[0][0] <= TILES * t + k:
-                    @pl.when(i == k)
-                    def _():
-                        if k == 3:
-                            tasks[t].run('up')
-                        advance(TILES * t + k)
-            return carry
-
-        lax.fori_loop(0, TILES, body, 0)
+        def segment(start, stop, mine):
+            def body(i, carry):
+                tile(i, mine, True)
+                for k in range(start, stop):
+                    if k == 3 or agenda and agenda[0][0] <= TILES * t + k:
+                        @pl.when(i == k)
+                        def _():
+                            events(k)
+                return carry
+
+            lax.fori_loop(start, stop, body, 0)
+
+        fetch(0)
+        for m in range(HALF // CHUNK):
+            front(0, m)
+        segment(0, RING, False)
+        segment(RING, TILES - 1, True)
+        tile(TILES - 1, True, False)
+        events(TILES - 1)
         if l == 1:
             cot[s] = (cot[s].astype(jnp.float32) + total[...]).astype(jnp.bfloat16)
         if t < 2:
@@ -373,30 +405,39 @@
         total[...] = jnp.zeros_like(total)
 
         def body(i, carry):
-            half, q, lane = lax.div(i, RING), lax.div(lax.rem(i, RING), 2), lax.rem(i, 2)
+            half, lane = lax.div(i, 2), lax.rem(i, 2)
             lanes = pl.ds(pl.multiple_of(lane * WIDTH, WIDTH), WIDTH)
-            raw = gath[t, half, :, :, :, :, lanes].astype(jnp.float32).reshape(64, ROWS, WIDTH)
-            w1 = jnp.where(q == 0, raw[:, 0:SUB], raw[:, SUB:ROWS]).reshape(DIM, WIDTH).astype(jnp.bfloat16)
-            rows = pl.ds(2 * lax.rem(i, 2), 2)
-            even = gath[t, 0, lax.div(i, 2), rows, :, :, DIM:HALF].reshape(SUB, 1, ROWS, DIM)
-            odd = gath[t, 1, lax.div(i, 2), rows, :, :, DIM:HALF].reshape(SUB, 1, ROWS, DIM)
-            w2 = jnp.concatenate([even, odd], axis=1).reshape(WIDTH, DIM)
-            h = mm(xbuf[s], w1, 1, 0)
-            tanh = jnp.tanh(h * (GELU_A + GELU_B * (h * h)))
-            act = (h * (0.5 * tanh + 0.5)).astype(jnp.bfloat16)
-            total[...] = total[...] + mm(act, w2, 1, 0)
-            for k in range(1, TILES, 2):
-                if agenda and agenda[0][0] <= now + k // 2:
+            raw = gath[t, half, :, :, :, :, lanes].astype(jnp.float32).reshape(RING ** 3, ROWS, WIDTH)
+            ups, downs = [], []
+            for q in range(2):
+                ups.append(raw[:, q * SUB:(q + 1) * SUB].reshape(DIM, WIDTH).astype(jnp.bfloat16))
+                rows = pl.ds(2 * lane, 2)
+                even = gath[t, 0, 2 * half + q, rows, :, :, DIM:HALF].reshape(SUB, 1, ROWS, DIM)
+                odd = gath[t, 1, 2 * half + q, rows, :, :, DIM:HALF].reshape(SUB, 1, ROWS, DIM)
+                downs.append(jnp.concatenate([even, odd], axis=1).reshape(WIDTH, DIM))
+            w1, w2 = jnp.concatenate(ups, axis=1), jnp.concatenate(downs, axis=0)
+            count = HALF // SPAN
+            hidden = mm(xbuf[s, 0:SPAN, :], w1, 1, 0)
+            for m in range(count):
+                h = hidden
+                if m + 1 < count:
+                    hidden = mm(xbuf[s, pl.ds((m + 1) * SPAN, SPAN), :], w1, 1, 0)
+                tanh = jnp.tanh(h * (GELU_A + GELU_B * (h * h)))
+                act = (h * (0.5 * tanh + 0.5)).astype(jnp.bfloat16)
+                span = pl.ds(m * SPAN, SPAN)
+                total[span, :] = total[span, :] + mm(act, w2, 1, 0)
+            for k in range(RING):
+                if agenda and agenda[0][0] <= now + k:
                     @pl.when(i == k)
                     def _():
-                        advance(now + k // 2)
+                        advance(now + k)
             return carry
 
-        lax.fori_loop(0, TILES, body, 0)
+        lax.fori_loop(0, RING, body, 0)
         xbuf[s] = (xbuf[s].astype(jnp.float32) + total[...]).astype(jnp.bfloat16)
         if l == 1:
             y_copy(s).start()
-        return now + TILES // 2
+        return now + RING
 
     for t in range(RING):
         backward(t)
@@ -421,6 +462,8 @@
         pltpu.VMEM((2, HALF, DIM), jnp.bfloat16),
         pltpu.VMEM((2, HALF, DIM), jnp.bfloat16),
         pltpu.VMEM((HALF, DIM), jnp.float32),
+        pltpu.VMEM((2, HALF, WIDTH), jnp.bfloat16),
+        pltpu.VMEM((2, HALF, WIDTH), jnp.bfloat16),
         pltpu.VMEM((RING,) * RING + (SUB, FF), jnp.float32),
         pltpu.VMEM((2, 2, 2, RING, SUB, FF), jnp.float32),
         pltpu.VMEM((2, 2, RING, RING, SUB, FF), jnp.float32),
@@ -447,12 +490,38 @@
     )(*args)
 
 
+def finish_kernel(*refs):
+    count = len(refs) // 3
+    sources, results, stage, sem = refs[:count], refs[count:2 * count], refs[2 * count:3 * count], refs[3 * count]
+    inward = [pltpu.make_async_copy(sources[i], stage[i], sem.at[0, i]) for i in range(count)]
+    outward = [pltpu.make_async_copy(stage[i], results[i], sem.at[1, i]) for i in range(count)]
+    for copy in inward:
+        copy.start()
+    for i in range(count):
+        inward[i].wait()
+        outward[i].start()
+    for copy in outward:
+        copy.wait()
+
+
+def finish(parts):
+    hbm = pl.BlockSpec(memory_space=pl.ANY)
+    return pl.pallas_call(
+        finish_kernel,
+        out_shape=tuple(jax.ShapeDtypeStruct(part.shape, part.dtype) for part in parts),
+        in_specs=[hbm] * len(parts),
+        out_specs=(hbm,) * len(parts),
+        scratch_shapes=[pltpu.VMEM(part.shape, part.dtype) for part in parts] + [pltpu.SemaphoreType.DMA((2, len(parts)))],
+        name='finish',
+    )(*parts)
+
+
 def solution(mesh):
     tok_spec = P(None, 'fsdp')
     layer_spec = P(None, None, 'fsdp')
     rep_spec = P()
 
     def device_step(*args):
-        return tuple(fused_step(*args))
+        return tuple(finish(fused_step(*args)))
 
     return jax.shard_map(device_step, mesh=mesh, in_specs=(layer_spec, tok_spec, tok_spec, rep_spec, rep_spec) + (layer_spec,) * SUB, out_specs=(layer_spec,) * 6 + (tok_spec,), check_vma=False)

time: 206 us -> 179 us (0.87)
  Pallas kernels: 192 us -> 178 us
  local copies, waits for them, and re-layouts: 12.4 us -> 0 us
    pallas_call x1, Pallas kernels: 192 us -> 174 us  [fused_step(): pl.pallas_call(step_kernel, out_shape=(up_state, down_state) * 3 + (jax.S...]
    unnamed x7 -> x0, local copies, waits for them, and re-layouts: 12.4 us -> none
    pallas_call x0 -> x1, Pallas kernels: none -> 3.51 us  [finish(): pl.pallas_call(finish_kernel, out_shape=tuple((jax.ShapeDtypeStruct(part....]
where the time goes in v3:
time: 179 us
  Pallas kernels  178 us (99%)
    pallas_call x1, Pallas kernels, fused_step(): pl.pallas_call(step_kernel, out_shape=(up_state, down_state) * 3 + (jax.S...  174 us

profile of v3, /device:TPU:1, one launch (start us, length us, event | category | flops | bytes accessed | tf_op | source)
XLA Modules:
  0.0 178.8 jit_solution(6493723457800369292)
XLA Ops:
  0.6 174.4 %step.1 = (f32[2,2,4,2048]{3,2,1,0:T(4,128)}, f32[2,2,16,512]{3,2,1,0:T(8,128)}, f32[2,2,4,2048]{3,2,1,0:T(4,128)}, f32[2,2,16,512]{3,2,1,0:T(8,128)}, f32[2,2,4...) custom-call(bf16[2,2,1,1024,512]{4,3,2,1,0:T(8,128)(2,1)} %refs_0_.1, ...), custom_call_target="tpu_custom_call" | custom-call | tf_op jit(solution)/shard_map/step/pallas_call | solution.py:482
  175.1 3.5 %finish.1 = (f32[2,2,4,2048]{3,2,1,0:T(4,128)}, f32[2,2,16,512]{3,2,1,0:T(8,128)}, f32[2,2,4,2048]{3,2,1,0:T(4,128)}, f32[2,2,16,512]{3,2,1,0:T(8,128)}, f32[2,2...) custom-call(f32[2,2,4,2048]{3,2,1,0:T(4,128)} %get-tuple-element.14.refs_0_, ...), custom_call_target="tpu_custom_call" | custom-call | tf_op jit(solution)/shard_map/finish/pallas_call | solution.py:509

commit v4 on v3

--- a/solution.py
+++ b/solution.py
@@ -15,8 +15,8 @@
 MESH = pl.DeviceIdType.MESH
 
 ORDERS = ((2, 1, 0), (1, 0, 2), (0, 2, 1))
-RS_LANES = ((0, 768), (768, 640), (1408, 640))
-AG_LANES = ((0, 384), (384, 384), (768, 256))
+RS_LANES = (((0, 384), (384, 384), (768, 256)), ((1024, 384), (1408, 256), (1664, 384)))
+AG_LANES = (((0, 128), (128, 128), (256, 256)), ((512, 128), (640, 256), (896, 128)))
 TASKS = ((0, 1), (0, 0), (1, 1), (1, 0))
 TILES = 8
 CHUNK = 512
@@ -28,7 +28,9 @@
 HALF = 1024
 FF = 2048
 WIDTH = 256
-OFFSETS = (0, 2, 6, 13, 17, 20, 21, 22, 24, 27, 32, 35, 39)
+GATHER_LAG = 4
+OFFSETS = ((0, 3, 8, 13, 18, 19, 20, 24, 28, 34, 38, 42),
+           (2, 6, 13, 18, 22, None, None, 26, 30, 36, 40, 44))
 FORWARD = ((1, 0, 0), (0, 0, 1), (3, 1, 0), (2, 1, 1))
 GELU_A = 0.7978845608028654
 GELU_B = GELU_A * 0.044715
@@ -70,6 +72,7 @@
     pos = (lax.div(chip, ROWS), lax.rem(lax.div(chip, RING), RING), lax.rem(chip, RING))
     stride = (32, SUB, 2)
     partner = me + 1 - 2 * core
+    near_z, far_z = 2 + core, 3 - core
     near = [[lax.rem(pos[axis] + step, RING) for step in range(RING)] for axis in range(3)]
     peers = [[me + (near[axis][step] - pos[axis]) * stride[axis] for step in range(RING)] for axis in range(3)]
 
@@ -114,20 +117,25 @@
             pl.semaphore_signal(barrier, inc=1, device_id=(peers[axis][step],), device_id_type=MESH)
     pl.semaphore_wait(barrier, 10)
 
-    class Task:
-        def __init__(self, task_id):
+    class Chain:
+        def __init__(self, task_id, part):
             self.t = task_id
             self.par = task_id % 2
+            self.part = part
+            self.row = 2 * task_id + part
             self.slot = 0
             self.live = []
             self.stage, self.layer = TASKS[task_id]
+            turn = [ORDERS[(g + task_id) % 3] for g in range(3)]
+            self.groups = [(g, turn[g], RS_LANES[part][g], AG_LANES[part][g]) for g in range(3)]
 
         def send(self, src, dst, device):
             slot = self.slot
             self.slot += 1
+            index = len(self.live)
 
             def make():
-                return pltpu.make_async_remote_copy(src_ref=src(), dst_ref=dst(), send_sem=send_sem.at[self.t, slot], recv_sem=recv_sem.at[self.t, slot], device_id=(device,), device_id_type=MESH)
+                return pltpu.make_async_remote_copy(src_ref=src(), dst_ref=dst(), send_sem=send_sem.at[self.row, index], recv_sem=recv_sem.at[self.row, slot], device_id=(device,), device_id_type=MESH)
 
             make().start()
             self.live.append(make)
@@ -137,20 +145,24 @@
                 make().wait()
             self.live = []
 
-        def plane_at(self, fixed, g):
-            return lambda: plane.at[(self.t,) + region(fixed, RS_LANES[g])]
-
-        def gath_at(self, fixed, g):
-            return lambda: gath.at[(self.t, core) + region(fixed, AG_LANES[g])]
+        def plane_at(self, fixed, span):
+            return lambda: plane.at[(self.t,) + region(fixed, span)]
+
+        def gath_at(self, fixed, span):
+            return lambda: gath.at[(self.t, core) + region(fixed, span)]
 
         def run(self, phase):
             getattr(self, 'phase_%s' % phase)()
 
-        def phase_up(self):
-            self.send(lambda: gath.at[self.t, 1, 0:2], lambda: gath.at[self.t, 0, 0:2], partner)
-
-        def phase_0(self):
-            self.send(lambda: gath.at[self.t, 1, 2:RING], lambda: gath.at[self.t, 0, 2:RING], partner)
+        def pass_half(self, z_blk):
+            self.send(lambda: gath.at[self.t, 1, z_blk], lambda: gath.at[self.t, 0, z_blk], partner)
+
+        def early(self):
+            self.pass_half(far_z if self.part else pl.ds(0, 2))
+
+        def late(self):
+            if self.part:
+                self.pass_half(near_z)
 
         def phase_1(self):
             t, par = self.t, self.par
@@ -159,151 +171,162 @@
             def body(i, carry):
                 z_pos, y_pos = lax.div(i, RING), lax.rem(i, RING)
                 z_blk, y_blk, x_blk = lax.div(i, SUB), lax.div(lax.rem(i, SUB), 2), 2 * lax.rem(i, 2)
-                up_part = gath[t, 0, z_blk, y_blk, pl.ds(x_blk, 2)].astype(jnp.float32)
-                plane[t, z_pos, y_pos, :, :, 0:HALF] = plane[t, z_pos, y_pos, :, :, 0:HALF] + up_part.reshape(RING, SUB, HALF)
-                down_part = gath[t, 0, z_blk + 2, y_blk, pl.ds(x_blk, 2)].astype(jnp.float32)
-                for k in range(2):
-                    for m in range(2):
-                        for h in range(2):
-                            lanes = slice(HALF + DIM * h, HALF + DIM * (h + 1))
-                            plane[t, z_pos, y_pos, 2 * k + m, :, lanes] = plane[t, z_pos, y_pos, 2 * k + m, :, lanes] + down_part[k, SUB * h:SUB * h + SUB, DIM * m:DIM * m + DIM]
+                got = gath[t, 0, z_blk + 2 * self.part, y_blk, pl.ds(x_blk, 2)].astype(jnp.float32)
+                if self.part == 0:
+                    plane[t, z_pos, y_pos, :, :, 0:HALF] = plane[t, z_pos, y_pos, :, :, 0:HALF] + got.reshape(RING, SUB, HALF)
+                else:
+                    for k in range(2):
+                        for m in range(2):
+                            for h in range(2):
+                                lanes = slice(HALF + DIM * h, HALF + DIM * (h + 1))
+                                plane[t, z_pos, y_pos, 2 * k + m, :, lanes] = plane[t, z_pos, y_pos, 2 * k + m, :, lanes] + got[k, SUB * h:SUB * (h + 1), DIM * m:DIM * (m + 1)]
                 return carry
 
             lax.fori_loop(0, ROWS, body, 0)
-            for g, order in enumerate(ORDERS):
+            for g, order, span, _ in self.groups:
                 axis, half = order[0], half_dim(order[0])
-                lanes = pl.ds(*RS_LANES[g])
+                lanes = pl.ds(*span)
                 for way, step in ((0, 1), (1, 3)):
-                    self.send(self.plane_at({axis: near[axis][2], half: pl.ds(2 * way, 2)}, g), lambda way=way, lanes=lanes: rs1.at[par, way, :, :, :, lanes], peers[axis][step])
+                    self.send(self.plane_at({axis: near[axis][2], half: pl.ds(2 * way, 2)}, span), lambda way=way, lanes=lanes: rs1.at[par, way, :, :, :, lanes], peers[axis][step])
 
         def phase_2(self):
             t, par = self.t, self.par
             self.drain()
-            for g, order in enumerate(ORDERS):
+            for g, order, span, _ in self.groups:
                 axis, half = order[0], half_dim(order[0])
-                lanes = pl.ds(*RS_LANES[g])
+                lanes = pl.ds(*span)
                 for way, step in ((0, 1), (1, 3)):
-                    where = (t,) + region({axis: near[axis][step], half: pl.ds(2 * way, 2)}, RS_LANES[g])
+                    where = (t,) + region({axis: near[axis][step], half: pl.ds(2 * way, 2)}, span)
                     plane[where] = plane[where] + rs1[par, way, :, :, :, lanes]
-            for g, order in enumerate(ORDERS):
+            for g, order, span, _ in self.groups:
                 axis = order[0]
-                lanes = pl.ds(*RS_LANES[g])
+                lanes = pl.ds(*span)
                 for way, step in ((0, 1), (1, 3)):
                     if t >= 2:
-                        pl.semaphore_wait(free_sem.at[0, par, g, way], 1)
-                    self.send(self.plane_at({axis: near[axis][step]}, g), lambda way=way, lanes=lanes: rs2.at[par, way, :, :, :, lanes], peers[axis][step])
+                        pl.semaphore_wait(free_sem.at[0, par, self.part, g, way], 1)
+                    self.send(self.plane_at({axis: near[axis][step]}, span), lambda way=way, lanes=lanes: rs2.at[par, way, :, :, :, lanes], peers[axis][step])
 
         def phase_3(self):
             t, par = self.t, self.par
             self.drain()
-            for g, order in enumerate(ORDERS):
-                lanes = pl.ds(*RS_LANES[g])
-                where = (t,) + region({order[0]: pos[order[0]]}, RS_LANES[g])
+            for g, order, span, _ in self.groups:
+                lanes = pl.ds(*span)
+                where = (t,) + region({order[0]: pos[order[0]]}, span)
                 plane[where] = plane[where] + (rs2[par, 0, :, :, :, lanes] + rs2[par, 1, :, :, :, lanes])
                 if t < 2:
                     for way, step in ((0, 3), (1, 1)):
-                        pl.semaphore_signal(free_sem.at[0, par, g, way], inc=1, device_id=(peers[order[0]][step],), device_id_type=MESH)
-            for g, order in enumerate(ORDERS):
-                lanes = pl.ds(*RS_LANES[g])
+                        pl.semaphore_signal(free_sem.at[0, par, self.part, g, way], inc=1, device_id=(peers[order[0]][step],), device_id_type=MESH)
+            for g, order, span, _ in self.groups:
+                lanes = pl.ds(*span)
                 axis = order[1]
                 for step in (1, 2, 3):
                     if t >= 2:
-                        pl.semaphore_wait(free_sem.at[1, par, g, step - 1], 1)
-                    self.send(self.plane_at({order[0]: pos[order[0]], axis: near[axis][step]}, g), lambda step=step, lanes=lanes: rs3.at[par, step - 1, :, :, lanes], peers[axis][step])
+                        pl.semaphore_wait(free_sem.at[1, par, self.part, g, step - 1], 1)
+                    self.send(self.plane_at({order[0]: pos[order[0]], axis: near[axis][step]}, span), lambda step=step, lanes=lanes: rs3.at[par, step - 1, :, :, lanes], peers[axis][step])
 
         def phase_4(self):
             t, par = self.t, self.par
             self.drain()
-            for g, order in enumerate(ORDERS):
-                lanes = pl.ds(*RS_LANES[g])
-                where = (t,) + region({order[0]: pos[order[0]], order[1]: pos[order[1]]}, RS_LANES[g])
+            for g, order, span, _ in self.groups:
+                lanes = pl.ds(*span)
+                where = (t,) + region({order[0]: pos[order[0]], order[1]: pos[order[1]]}, span)
                 plane[where] = plane[where] + (rs3[par, 0, :, :, lanes] + rs3[par, 1, :, :, lanes] + rs3[par, 2, :, :, lanes])
                 if t < 2:
                     for step in (1, 2, 3):
-                        pl.semaphore_signal(free_sem.at[1, par, g, step - 1], inc=1, device_id=(peers[order[1]][RING - step],), device_id_type=MESH)
-            for g, order in enumerate(ORDERS):
-                lanes = pl.ds(*RS_LANES[g])
+                        pl.semaphore_signal(free_sem.at[1, par, self.part, g, step - 1], inc=1, device_id=(peers[order[1]][RING - step],), device_id_type=MESH)
+            for g, order, span, _ in self.groups:
+                lanes = pl.ds(*span)
                 axis = order[2]
                 fixed = {order[0]: pos[order[0]], order[1]: pos[order[1]]}
                 for step in (1, 2, 3):
-                    self.send(self.plane_at({**fixed, axis: near[axis][step]}, g), lambda step=step, lanes=lanes: rs4.at[t, step - 1, :, lanes], peers[axis][step])
+                    self.send(self.plane_at({**fixed, axis: near[axis][step]}, span), lambda step=step, lanes=lanes: rs4.at[t, step - 1, :, lanes], peers[axis][step])
 
         def phase_5(self):
             t = self.t
             self.drain()
-            block = plane[t, pos[0], pos[1], pos[2]] + (rs4[t, 0] + rs4[t, 1] + rs4[t, 2])
-            block8[t] = block
-            grad_x[t, core] = block[:, 0:HALF]
-            self.send(lambda: grad_x.at[t, core], lambda: grad_x.at[t, core], partner)
+            lanes = slice(HALF * self.part, HALF * (self.part + 1))
+            block = plane[t, pos[0], pos[1], pos[2], :, lanes] + (rs4[t, 0, :, lanes] + rs4[t, 1, :, lanes] + rs4[t, 2, :, lanes])
+            if self.part == 0:
+                grad_x[t, core] = block
+                self.send(lambda: grad_x.at[t, core], lambda: grad_x.at[t, core], partner)
+            else:
+                s, l = self.stage, self.layer
+                grad = jnp.concatenate([block[:, 0:DIM], block[:, DIM:HALF]], axis=0)
+                new = adam_update(acc_down[s, l], grad, master_down[s, l], m1_down[s, l], m2_down[s, l])
+                for i in range(3):
+                    out_states[2 * i + 1][s, l] = new[i]
+                gath[t, core, pos[0], pos[1], pos[2], :, DIM:HALF] = new[0].astype(jnp.bfloat16)
+                self.spread()
 
         def phase_6(self):
             t, s, l = self.t, self.stage, self.layer
             self.drain()
-            grad_down = jnp.concatenate([block8[t, :, HALF:HALF + DIM], block8[t, :, HALF + DIM:FF]], axis=0)
-            new_down = adam_update(acc_down[s, l], grad_down, master_down[s, l], m1_down[s, l], m2_down[s, l])
             low = jnp.concatenate([grad_x[t, 0, 0:RING, :], grad_x[t, 1, 0:RING, :]], axis=1)
             high = jnp.concatenate([grad_x[t, 0, RING:SUB, :], grad_x[t, 1, RING:SUB, :]], axis=1)
             grad_up = jnp.where(core == 0, low, high)
             new_up = adam_update(acc_up[s, l], grad_up, master_up[s, l], m1_up[s, l], m2_up[s, l])
             for i in range(3):
                 out_states[2 * i][s, l] = new_up[i]
-                out_states[2 * i + 1][s, l] = new_down[i]
             left, right = new_up[0][:, 0:HALF], new_up[0][:, HALF:FF]
             part_x[t, core] = jnp.where(core == 0, left, right)
             part_x[t, 2] = jnp.where(core == 0, right, left)
             self.send(lambda: part_x.at[t, 2], lambda: part_x.at[t, core], partner)
-            gath[t, core, pos[0], pos[1], pos[2], :, DIM:HALF] = new_down[0].astype(jnp.bfloat16)
 
         def phase_7(self):
             t = self.t
             self.drain()
-            block8[t, 0:RING, 0:HALF] = part_x[t, 0]
-            block8[t, RING:SUB, 0:HALF] = part_x[t, 1]
+            block8[t, 0:RING, :] = part_x[t, 0]
+            block8[t, RING:SUB, :] = part_x[t, 1]
             rows = jnp.concatenate([block8[t, :, 0:DIM], block8[t, :, DIM:HALF]], axis=0)
             gath[t, core, pos[0], pos[1], pos[2], :, 0:DIM] = rows.astype(jnp.bfloat16)
-            for g, order in enumerate(ORDERS):
-                where = self.gath_at({0: pos[0], 1: pos[1], 2: pos[2]}, g)
+            self.spread()
+
+        def spread(self):
+            for g, order, _, span in self.groups:
+                where = self.gath_at({0: pos[0], 1: pos[1], 2: pos[2]}, span)
                 for step in (1, 2, 3):
                     self.send(where, where, peers[order[2]][step])
 
         def phase_8(self):
             self.drain()
-            for g, order in enumerate(ORDERS):
-                where = self.gath_at({order[0]: pos[order[0]], order[1]: pos[order[1]]}, g)
+            for g, order, _, span in self.groups:
+                where = self.gath_at({order[0]: pos[order[0]], order[1]: pos[order[1]]}, span)
                 for step in (1, 2, 3):
                     self.send(where, where, peers[order[1]][step])
 
         def phase_9(self):
             self.drain()
-            for g, order in enumerate(ORDERS):
-                where = self.gath_at({order[0]: pos[order[0]]}, g)
+            for g, order, _, span in self.groups:
+                where = self.gath_at({order[0]: pos[order[0]]}, span)
                 for step in (1, 3):
                     self.send(where, where, peers[order[0]][step])
 
         def phase_10(self):
             self.drain()
-            for g, order in enumerate(ORDERS):
+            for g, order, _, span in self.groups:
                 axis, half = order[0], half_dim(order[0])
                 for way, step in ((0, 1), (1, 3)):
-                    where = self.gath_at({axis: near[axis][RING - step], half: pl.ds(2 * way, 2)}, g)
+                    where = self.gath_at({axis: near[axis][RING - step], half: pl.ds(2 * way, 2)}, span)
                     self.send(where, where, peers[axis][step])
 
         def phase_11(self):
             self.drain()
-            self.send(lambda: gath.at[self.t, core], lambda: gath.at[self.t, core], partner)
+            lanes = pl.ds(DIM * self.part, DIM)
+            whole = lambda: gath.at[self.t, core, :, :, :, :, lanes]
+            self.send(whole, whole, partner)
 
         def phase_12(self):
             self.drain()
 
-    tasks = [Task(t) for t in range(RING)]
-    agenda = sorted((TILES * (t + 1) - 1 + offset, t, phase) for t in range(RING) for phase, offset in enumerate(OFFSETS))
+    chains = [[Chain(t, part) for part in range(2)] for t in range(RING)]
+    agenda = sorted((TILES * (t + 1) - 1 + offset + (GATHER_LAG * (3 - t) if phase > 5 else 0), t, part, phase + 1) for t in range(RING) for part in range(2) for phase, offset in enumerate(OFFSETS[part]) if offset is not None)
     finished = set()
 
     def advance(now):
         while agenda and agenda[0][0] <= now:
-            _, t, phase = agenda.pop(0)
-            tasks[t].run(phase)
-            finished.add((t, phase))
+            _, t, part, phase = agenda.pop(0)
+            chains[t][part].run(phase)
+            finished.add((t, part, phase))
 
     def backward(t):
         s, l = TASKS[t]
@@ -354,7 +377,11 @@
 
         def events(k):
             if k == 3:
-                tasks[t].run('up')
+                for chain in chains[t]:
+                    chain.early()
+            if k == TILES - 1:
+                for chain in chains[t]:
+                    chain.late()
             advance(TILES * t + k)
 
         def tile(i, mine, ahead):
@@ -443,7 +470,7 @@
         backward(t)
     now = RING * TILES - 1
     for t, s, l in FORWARD:
-        while (t, 12) not in finished:
+        while not finished >= {(t, 0, 12), (t, 1, 12)}:
             now = max(now, agenda[0][0])
             advance(agenda[0][0])
         now = forward(t, s, l, now)
@@ -471,13 +498,13 @@
         pltpu.VMEM((RING, 3, SUB, FF), jnp.float32),
         pltpu.VMEM((RING, 2, SUB, HALF), jnp.float32),
         pltpu.VMEM((RING, 3, RING, HALF), jnp.float32),
-        pltpu.VMEM((RING, SUB, FF), jnp.float32),
+        pltpu.VMEM((RING, SUB, HALF), jnp.float32),
         pltpu.VMEM((RING, 2, RING, RING, RING, ROWS, HALF), jnp.bfloat16),
         pltpu.SemaphoreType.DMA((2, TILES)),
         pltpu.SemaphoreType.DMA((6,)),
-        pltpu.SemaphoreType.DMA((RING, 66)),
-        pltpu.SemaphoreType.DMA((RING, 66)),
-        pltpu.SemaphoreType.REGULAR((2, 2, 3, 3)),
+        pltpu.SemaphoreType.DMA((SUB, 9)),
+        pltpu.SemaphoreType.DMA((SUB, 66)),
+        pltpu.SemaphoreType.REGULAR((2, 2, 2, 3, 3)),
     ]
     return pl.pallas_call(
         step_kernel,

time: 179 us -> 169 us (0.944)
  Pallas kernels: 178 us -> 168 us
    pallas_call x1, Pallas kernels: 174 us -> 164 us  [fused_step(): pl.pallas_call(step_kernel, out_shape=(up_state, down_state) * 3 + (jax.S...]
where the time goes in v4:
time: 169 us
  Pallas kernels  168 us (99%)
    pallas_call x1, Pallas kernels, fused_step(): pl.pallas_call(step_kernel, out_shape=(up_state, down_state) * 3 + (jax.S...  164 us
    pallas_call x1, Pallas kernels, finish(): pl.pallas_call(finish_kernel, out_shape=tuple((jax.ShapeDtypeStruct(part....  3.51 us

profile of v4, /device:TPU:1, one launch (start us, length us, event | category | flops | bytes accessed | tf_op | source)
XLA Modules:
  0.0 168.5 jit_solution(11863296738467821685)
XLA Ops:
  0.6 164.2 %step.1 = (f32[2,2,4,2048]{3,2,1,0:T(4,128)}, f32[2,2,16,512]{3,2,1,0:T(8,128)}, f32[2,2,4,2048]{3,2,1,0:T(4,128)}, f32[2,2,16,512]{3,2,1,0:T(8,128)}, f32[2,2,4...) custom-call(bf16[2,2,1,1024,512]{4,3,2,1,0:T(8,128)(2,1)} %refs_0_.1, ...), custom_call_target="tpu_custom_call" | custom-call | tf_op jit(solution)/shard_map/step/pallas_call | solution.py:509
  164.8 3.5 %finish.1 = (f32[2,2,4,2048]{3,2,1,0:T(4,128)}, f32[2,2,16,512]{3,2,1,0:T(8,128)}, f32[2,2,4,2048]{3,2,1,0:T(4,128)}, f32[2,2,16,512]{3,2,1,0:T(8,128)}, f32[2,2...) custom-call(f32[2,2,4,2048]{3,2,1,0:T(4,128)} %get-tuple-element.14.refs_0_, ...), custom_call_target="tpu_custom_call" | custom-call | tf_op jit(solution)/shard_map/finish/pallas_call | solution.py:536

commit v5 on v4

--- a/solution.py
+++ b/solution.py
@@ -20,7 +20,7 @@
 TASKS = ((0, 1), (0, 0), (1, 1), (1, 0))
 TILES = 8
 CHUNK = 512
-SPAN = 256
+SPAN = 512
 RING = 4
 SUB = 8
 ROWS = 16
@@ -29,8 +29,8 @@
 FF = 2048
 WIDTH = 256
 GATHER_LAG = 4
-OFFSETS = ((0, 3, 8, 13, 18, 19, 20, 24, 28, 34, 38, 42),
-           (2, 6, 13, 18, 22, None, None, 26, 30, 36, 40, 44))
+OFFSETS = ((0, 3, 8, 13, 17, 18, 19, 22, 26, 31, 35, 39),
+           (1, 5, 11, 16, 20, None, None, 24, 28, 33, 37, 41))
 FORWARD = ((1, 0, 0), (0, 0, 1), (3, 1, 0), (2, 1, 1))
 GELU_A = 0.7978845608028654
 GELU_B = GELU_A * 0.044715

time: 169 us -> 166 us (0.982)
  Pallas kernels: 168 us -> 164 us
    pallas_call x1, Pallas kernels: 164 us -> 160 us  [fused_step(): pl.pallas_call(step_kernel, out_shape=(up_state, down_state) * 3 + (jax.S...]
where the time goes in v5:
time: 166 us; the launch traced here: 165 us
  Pallas kernels  164 us (99%)
    pallas_call x1, Pallas kernels, fused_step(): pl.pallas_call(step_kernel, out_shape=(up_state, down_state) * 3 + (jax.S...  160 us
    pallas_call x1, Pallas kernels, finish(): pl.pallas_call(finish_kernel, out_shape=tuple((jax.ShapeDtypeStruct(part....  3.51 us

profile of v5, /device:TPU:1, one launch (start us, length us, event | category | flops | bytes accessed | tf_op | source)
XLA Modules:
  0.0 164.7 jit_solution(7267747027336884258)
XLA Ops:
  0.6 160.4 %step.1 = (f32[2,2,4,2048]{3,2,1,0:T(4,128)}, f32[2,2,16,512]{3,2,1,0:T(8,128)}, f32[2,2,4,2048]{3,2,1,0:T(4,128)}, f32[2,2,16,512]{3,2,1,0:T(8,128)}, f32[2,2,4...) custom-call(bf16[2,2,1,1024,512]{4,3,2,1,0:T(8,128)(2,1)} %refs_0_.1, ...), custom_call_target="tpu_custom_call" | custom-call | tf_op jit(solution)/shard_map/step/pallas_call | solution.py:509
  161.0 3.5 %finish.1 = (f32[2,2,4,2048]{3,2,1,0:T(4,128)}, f32[2,2,16,512]{3,2,1,0:T(8,128)}, f32[2,2,4,2048]{3,2,1,0:T(4,128)}, f32[2,2,16,512]{3,2,1,0:T(8,128)}, f32[2,2...) custom-call(f32[2,2,4,2048]{3,2,1,0:T(4,128)} %get-tuple-element.14.refs_0_, ...), custom_call_target="tpu_custom_call" | custom-call | tf_op jit(solution)/shard_map/finish/pallas_call | solution.py:536
